TPU v7x, 32 devices: a whole 2x2x4 slice. The times are simulated.
32 devices in a mesh: prompt: 4 (over x, core), dp: 4 (over z), mp: 2 (over y).
Axes of the slice: x: 2, y: 2, z: 4, core: 2. Of those that a mesh axis runs over, the one named last changes fastest.
Arguments:
- prompts: bfloat16 [8, 100, 4096], P('prompt'), may hold values from -6 to 6
- target_embed: bfloat16 [4, 512, 4096], P('dp'), may hold values from -6 to 6
- labels: int32 [4, 512], P('dp'), may hold values from 0 to 16383
- lengths: int32 [4], P('dp'), may hold values from 128 to 512
- attn_gain: float32 [4096], replicated, may hold values from 0.5 to 1.5
- w_qkv: bfloat16 [3, 4096, 2048], P(None, None, 'mp'), may hold values from -4 to 4
- w_out: bfloat16 [2048, 4096], P('mp'), may hold values from -0.5 to 0.5
- final_gain: float32 [4096], replicated, may hold values from 0.5 to 1.5
- w_vocab: bfloat16 [4096, 16384], P(None, ('dp', 'mp')), may hold values from -3 to 3
Outputs:
- token_loss: float32 [8, 4, 512], P('prompt', 'dp')
- prompt_loss: float32 [8], replicated
Inputs may be any that keep to these rules, and one draw needn't show every extreme that they name: `lengths`: positions from a sequence's length on are padding.
All inputs are finite; a program needn't handle non-finite values.
Results may differ from a plain program's by a relative error of at most 0.006.
Values may be sent and summed in bfloat16 or wider, within the bound.
A program may use at most 192 MiB of HBM per device.

v0:
```python
import functools
import math

import jax
import jax.numpy as jnp
from jax import lax
from jax.experimental import pallas as pl
from jax.experimental.pallas import tpu as pltpu
from jax.sharding import PartitionSpec as P


HD = 128
EPSILON = 1e-05
BASE_THETA = 10000.0
LANES = 128
NEG = -1e30


def shift_by(value, axis, hop):
    size = lax.axis_size(axis)
    return lax.ppermute(value, axis, [(i, (i + hop) % size) for i in range(size)])


def ring_source(axis, hop):
    size = lax.axis_size(axis)
    return lax.rem(lax.axis_index(axis) + size - hop, size)


def in_order(parts, axis):
    size = len(parts)
    stacked = jnp.stack(parts)
    owners = lax.axis_index(axis) + size - jnp.arange(size, dtype=jnp.int32)
    return jnp.take(stacked, lax.rem(owners, size), axis=0)


def small_gather(value, axis):
    size = lax.axis_size(axis)
    return in_order([value] + [shift_by(value, axis, k) for k in range(1, size)], axis)


def spread(piece, axis):
    size = lax.axis_size(axis)
    me = lax.axis_index(axis)
    if size & (size - 1):
        return [(piece, me)] + [(shift_by(piece, axis, k), ring_source(axis, k)) for k in range(1, size)]
    held = [(piece, me)]
    bit = size // 2
    while bit:
        pairs = [(i, i ^ bit) for i in range(size)]
        held = held + [
            (lax.ppermute(part, axis, pairs), jnp.bitwise_xor(owner, bit)) for part, owner in held
        ]
        bit //= 2
    return held


def assemble(held):
    height = held[0][0].shape[0]
    whole = jnp.zeros((len(held) * height,) + held[0][0].shape[1:], held[0][0].dtype)
    for part, owner in held:
        whole = lax.dynamic_update_slice_in_dim(whole, part, owner * height, 0)
    return whole


def peer_piece(array, axis):
    height = array.shape[0] // lax.axis_size(axis)
    return lax.dynamic_slice_in_dim(array, lax.axis_index(axis) * height, height, 0)


def rope_tables(positions):
    half = HD // 2
    frequency = jnp.exp(
        jnp.arange(half, dtype=jnp.int32).astype(jnp.float32) * (-2.0 * math.log(BASE_THETA) / HD)
    )
    angles = positions.astype(jnp.float32)[:, None] * frequency[None, :]
    cosine, sine = jnp.cos(angles), jnp.sin(angles)
    return jnp.concatenate([cosine, cosine], 1), jnp.concatenate([-sine, sine], 1)


def largest_tile(width, most):
    tile = min(width, most)
    while width % tile:
        tile -= LANES
    return tile


def qkv_body(rows_target, target_ref, prompt_ref, gain_ref, w_ref, cos_ref, sin_ref, out_ref, normed):
    which = pl.program_id(0)

    @pl.when((which == 0) & (pl.program_id(1) == 0))
    def _():
        for ref, start in ((target_ref, 0), (prompt_ref, rows_target)):
            step = 64

            def one(i, carry, ref=ref, start=start):
                lo = pl.multiple_of(i * step, step)
                wide = ref[pl.ds(lo, step), :].astype(jnp.float32)
                scale = lax.rsqrt(jnp.mean(wide * wide, axis=-1, keepdims=True) + EPSILON)
                normed[pl.ds(pl.multiple_of(start + lo, step), step), :] = (
                    wide * scale * gain_ref[...]
                ).astype(jnp.bfloat16)
                return carry

            lax.fori_loop(0, ref.shape[0] // step, one, 0)

    total = normed.shape[0]
    block = 256

    def rows(lo, turn):
        acc = jnp.dot(
            normed[lo : lo + block, :], w_ref[0], preferred_element_type=jnp.float32
        )
        for h in range(acc.shape[1] // HD):
            part = acc[:, h * HD : (h + 1) * HD]
            if turn:
                part = part * cos_ref[lo : lo + block, :] + pltpu.roll(part, HD // 2, 1) * sin_ref[lo : lo + block, :]
            out_ref[0, lo : lo + block, h * HD : (h + 1) * HD] = part.astype(jnp.bfloat16)

    @pl.when(which == 0)
    def _():
        for lo in range(0, rows_target, block):
            rows(lo, True)
        out_ref[0, rows_target:, :] = jnp.zeros((total - rows_target, out_ref.shape[2]), jnp.bfloat16)

    @pl.when(which == 1)
    def _():
        for lo in range(0, total, block):
            rows(lo, True)

    @pl.when(which == 2)
    def _():
        for lo in range(0, total, block):
            rows(lo, False)


def project(target_rows, prompt_rows, gain, w_qkv, cosine, sine):
    rows_target, depth = target_rows.shape
    total = rows_target + prompt_rows.shape[0]
    width = w_qkv.shape[2]
    tile = largest_tile(width, 512)
    return pl.pallas_call(
        functools.partial(qkv_body, rows_target),
        grid=(3, width // tile),
        in_specs=[
            pl.BlockSpec((rows_target, depth), lambda c, j: (0, 0)),
            pl.BlockSpec(prompt_rows.shape, lambda c, j: (0, 0)),
            pl.BlockSpec((1, depth), lambda c, j: (0, 0)),
            pl.BlockSpec((1, depth, tile), lambda c, j: (c, 0, j)),
            pl.BlockSpec((total, HD), lambda c, j: (0, 0)),
            pl.BlockSpec((total, HD), lambda c, j: (0, 0)),
        ],
        out_specs=pl.BlockSpec((1, total, tile), lambda c, j: (c, 0, j)),
        out_shape=jax.ShapeDtypeStruct((3, total, width), jnp.bfloat16),
        scratch_shapes=[pltpu.VMEM((total, depth), jnp.bfloat16)],
        cost_estimate=pl.CostEstimate(
            flops=6 * total * depth * width, bytes_accessed=6 * depth * width, transcendentals=0
        ),
        name="qkv_rope",
    )(target_rows, prompt_rows, gain.reshape(1, -1), w_qkv, cosine, sine)


def attend_body(prompts_here, target_len, seqs, prompt_len, pad_len, q_ref, k_ref, v_ref, out_ref):
    scale = HD ** (-0.5)
    block = 256 if target_len % 256 == 0 else target_len
    rows_target = seqs * target_len
    contract = (((1,), (1,)), ((), ()))
    col = lax.broadcasted_iota(jnp.int32, (block, pad_len), 1)
    for b in range(seqs):
        base = b * target_len
        for i in range(target_len // block):
            lo = base + i * block
            reach = (i + 1) * block
            query = q_ref[0, lo : lo + block, :]
            s = lax.dot_general(
                query, k_ref[0, base : base + reach, :], contract, preferred_element_type=jnp.float32
            ) * scale
            row_id = lax.broadcasted_iota(jnp.int32, s.shape, 0) + i * block
            col_id = lax.broadcasted_iota(jnp.int32, s.shape, 1)
            s = jnp.where(col_id <= row_id, s, NEG)
            top = jnp.max(s, axis=1, keepdims=True)
            p = jnp.exp(s - top)
            mass = jnp.sum(p, axis=1, keepdims=True)
            own = jnp.dot(
                p.astype(jnp.bfloat16), v_ref[0, base : base + reach, :], preferred_element_type=jnp.float32
            )
            for j in range(prompts_here):
                at = rows_target + j * pad_len
                s1 = lax.dot_general(
                    query, k_ref[0, at : at + pad_len, :], contract, preferred_element_type=jnp.float32
                ) * scale
                s1 = jnp.where(col < prompt_len, s1, NEG)
                peak = jnp.maximum(top, jnp.max(s1, axis=1, keepdims=True))
                p1 = jnp.exp(s1 - peak)
                keep = jnp.exp(top - peak)
                whole = mass * keep + jnp.sum(p1, axis=1, keepdims=True)
                got = own * keep + jnp.dot(
                    p1.astype(jnp.bfloat16), v_ref[0, at : at + pad_len, :], preferred_element_type=jnp.float32
                )
                out_ref[j, lo : lo + block, :] = (got / whole).astype(jnp.bfloat16)


def attend(qkv, prompts_here, target_len, seqs, prompt_len, pad_len):
    total, width = qkv.shape[1:]
    heads = width // HD
    rows_target = seqs * target_len
    return pl.pallas_call(
        functools.partial(attend_body, prompts_here, target_len, seqs, prompt_len, pad_len),
        grid=(heads,),
        in_specs=[
            pl.BlockSpec((1, total, HD), lambda h, c=c: (c, 0, h)) for c in range(3)
        ],
        out_specs=pl.BlockSpec((prompts_here, rows_target, HD), lambda h: (0, 0, h)),
        out_shape=jax.ShapeDtypeStruct((prompts_here, rows_target, width), jnp.bfloat16),
        cost_estimate=pl.CostEstimate(
            flops=10 * heads * rows_target * target_len * HD, bytes_accessed=8 * total * width, transcendentals=0
        ),
        name="attend",
    )(qkv, qkv, qkv)


def out_body(piece_count, owners_ref, ctx_ref, other_ref, embed_ref, gain_ref, w_ref, *rest):
    piece_refs = rest[:piece_count]
    out_ref, hidden, squares, turned = rest[piece_count:]
    j = pl.program_id(0)
    tile = w_ref.shape[1]
    rows = ctx_ref.shape[0]

    @pl.when(j == 0)
    def _():
        low = 0
        for n, ref in enumerate(piece_refs):
            high = ref.shape[0]
            at = pl.multiple_of(owners_ref[n], 128)
            turned[:, low : low + high] = other_ref[:, pl.ds(at, high)]
            low += high
        squares[...] = jnp.zeros(squares.shape, jnp.float32)

    weights = jnp.concatenate([ref[...] for ref in piece_refs], axis=0)
    block = 256 if rows % 256 == 0 else rows
    for lo in range(0, rows, block):
        acc = jnp.dot(ctx_ref[lo : lo + block, :], w_ref[...], preferred_element_type=jnp.float32)
        acc += jnp.dot(turned[lo : lo + block, :], weights, preferred_element_type=jnp.float32)
        acc += embed_ref[lo : lo + block, :].astype(jnp.float32)
        hidden[j, lo : lo + block, :] = acc
        part = acc[:, :LANES] * acc[:, :LANES]
        for g in range(LANES, tile, LANES):
            part += acc[:, g : g + LANES] * acc[:, g : g + LANES]
        squares[lo : lo + block, :] += part

    @pl.when(j == pl.num_programs(0) - 1)
    def _():
        steps = hidden.shape[0]
        mean = jnp.sum(squares[...], axis=1, keepdims=True) / (steps * tile)
        scale = lax.rsqrt(mean + EPSILON)
        for n in range(steps):
            out_ref[:, n * tile : (n + 1) * tile] = (
                hidden[n] * scale * gain_ref[:, n * tile : (n + 1) * tile]
            ).astype(jnp.bfloat16)


def out_project(ctx, other, embed, gain, w_own, pieces, offsets):
    total, depth = ctx.shape
    width = w_own.shape[1]
    tile = largest_tile(width, 512)
    rows = total
    line = lambda j, *_: (0, 0)
    column = lambda j, *_: (0, j)
    return pl.pallas_call(
        functools.partial(out_body, len(pieces)),
        grid_spec=pltpu.PrefetchScalarGridSpec(
            num_scalar_prefetch=1,
            grid=(width // tile,),
            in_specs=[
                pl.BlockSpec((rows, depth), line),
                pl.BlockSpec((rows, other.shape[1]), line),
                pl.BlockSpec((rows, tile), lambda j, *_: (0, j)),
                pl.BlockSpec((1, width), lambda j, *_: (0, 0)),
                pl.BlockSpec((w_own.shape[0], tile), column),
            ]
            + [pl.BlockSpec((piece.shape[0], tile), column) for piece in pieces],
            out_specs=pl.BlockSpec((rows, width), line),
            scratch_shapes=[
                pltpu.VMEM((width // tile, rows, tile), jnp.float32),
                pltpu.VMEM((rows, LANES), jnp.float32),
                pltpu.VMEM((rows, other.shape[1]), jnp.bfloat16),
            ],
        ),
        out_shape=jax.ShapeDtypeStruct((total, width), jnp.bfloat16),
        cost_estimate=pl.CostEstimate(
            flops=2 * total * (depth + other.shape[1]) * width, bytes_accessed=4 * depth * width, transcendentals=0
        ),
        name="out_project",
    )(offsets, ctx, other, embed, gain.reshape(1, -1), w_own, *pieces)


def vocab_body(piece_count, scalars_ref, rows_ref, labels_ref, top_in, mass_in, pick_in, *rest):
    piece_refs = rest[:piece_count]
    top_ref, mass_ref, pick_ref = rest[piece_count:]
    j = pl.program_id(0)
    tile = piece_refs[0].shape[1]
    rows = rows_ref.shape[0]

    @pl.when(j == 0)
    def _():
        top_ref[...] = top_in[...]
        mass_ref[...] = mass_in[...]
        pick_ref[...] = pick_in[...]

    first = scalars_ref[0] + j * tile
    block = 256 if rows % 256 == 0 else rows
    for lo in range(0, rows, block):
        acc = None
        for n, ref in enumerate(piece_refs):
            high = ref.shape[0]
            if piece_count == 1:
                left = rows_ref[lo : lo + block, :]
            else:
                at = pl.multiple_of(scalars_ref[1 + n], 128)
                left = rows_ref[lo : lo + block, pl.ds(at, high)]
            part = jnp.dot(left, ref[...], preferred_element_type=jnp.float32)
            acc = part if acc is None else acc + part
        wanted = labels_ref[lo : lo + block, :] - first
        lane = lax.broadcasted_iota(jnp.int32, (block, LANES), 1)
        groups = [acc[:, g : g + LANES] for g in range(0, tile, LANES)]
        before = top_ref[lo : lo + block, :]
        now = before
        for g in groups:
            now = jnp.maximum(now, g)
        mass = mass_ref[lo : lo + block, :] * jnp.exp(before - now)
        pick = pick_ref[lo : lo + block, :]
        for n, g in enumerate(groups):
            mass += jnp.exp(g - now)
            pick += jnp.where(lane == wanted - n * LANES, g, 0.0)
        top_ref[lo : lo + block, :] = now
        mass_ref[lo : lo + block, :] = mass
        pick_ref[lo : lo + block, :] = pick


def vocab_stats(normed, labels, pieces, scalars, stats):
    rows, depth = normed.shape
    width = pieces[0].shape[1]
    tile = largest_tile(width, 512)
    fixed = lambda j, *_: (0, 0)
    lanes = pl.BlockSpec((rows, LANES), fixed)
    return pl.pallas_call(
        functools.partial(vocab_body, len(pieces)),
        grid_spec=pltpu.PrefetchScalarGridSpec(
            num_scalar_prefetch=1,
            grid=(width // tile,),
            in_specs=[pl.BlockSpec((rows, depth), fixed), pl.BlockSpec((rows, 1), fixed)]
            + [lanes] * 3
            + [pl.BlockSpec((piece.shape[0], tile), lambda j, *_: (0, j)) for piece in pieces],
            out_specs=[lanes] * 3,
        ),
        out_shape=[jax.ShapeDtypeStruct((rows, LANES), jnp.float32)] * 3,
        cost_estimate=pl.CostEstimate(
            flops=2 * rows * depth * width, bytes_accessed=2 * depth * width, transcendentals=0
        ),
        name="vocab_stats",
    )(scalars, normed, labels.reshape(-1, 1), *stats, *pieces)


def fresh_stats(rows):
    zero = jnp.zeros((rows, LANES), jnp.float32)
    return (jnp.full((rows, LANES), NEG, jnp.float32), zero, zero)


def fold_lanes(stats):
    top, mass, pick = stats
    peak = jnp.max(top, axis=1)
    return jnp.stack([peak, jnp.sum(mass * jnp.exp(top - peak[:, None]), axis=1), jnp.sum(pick, axis=1)])


def combine_stats(earlier, later):
    top_val = jnp.maximum(earlier[0], later[0])
    sum_exp = earlier[1] * jnp.exp(earlier[0] - top_val) + later[1] * jnp.exp(later[0] - top_val)
    return jnp.stack((top_val, sum_exp, earlier[2] + later[2]))


def swap_pair(value, axis):
    size = lax.axis_size(axis)
    return lax.ppermute(value, axis, [(i, i ^ 1) for i in range(size)])


def shards(prompts, target_embed, labels, lengths, attn_gain, w_qkv, w_out, final_gain, w_vocab):
    n_model = lax.axis_size("mp")
    n_seq = lax.axis_size("dp")
    my_seq = lax.axis_index("dp")
    prompts_here, prompt_len, model_width = prompts.shape
    seq_count, target_len, _ = target_embed.shape
    hops = range(1, n_model)
    paired = n_seq % 2 == 0
    stride = 2 if paired else 1
    unit = seq_count * target_len

    got_out = []
    for k in hops:
        got_out.append(shift_by(peer_piece(w_out, "prompt"), "mp", k))
    flat_embed = target_embed.reshape(-1, model_width)
    if paired:
        got_embed = swap_pair(peer_piece(flat_embed, "prompt"), "dp")
    parts = 4 if w_vocab.shape[1] % 512 == 0 else 1
    part_cols = w_vocab.shape[1] // parts
    vocab_jobs = [(k, c) for k in range(stride, n_seq, stride) for c in range(parts)]
    own_piece = peer_piece(w_vocab, "prompt")

    def fetch(n):
        k, c = vocab_jobs[n]
        return shift_by(own_piece[:, c * part_cols : (c + 1) * part_cols], "dp", k)

    got_vocab = [fetch(0)]

    pad_len = -(-prompt_len // 128) * 128
    positions = jnp.concatenate(
        [prompt_len + jnp.arange(target_len, dtype=jnp.int32)] * seq_count
        + [jnp.arange(pad_len, dtype=jnp.int32)] * prompts_here
    )
    cosine, sine = rope_tables(positions)
    padded = jnp.pad(prompts, ((0, 0), (0, pad_len - prompt_len), (0, 0))).reshape(-1, model_width)
    qkv = project(flat_embed, padded, attn_gain, w_qkv, cosine, sine)
    ctx = attend(qkv, prompts_here, target_len, seq_count, prompt_len, pad_len)
    ctx = ctx.reshape(prompts_here * unit, -1)

    if paired:
        ctx_pair = swap_pair(ctx, "dp")
    other_a = jnp.concatenate([shift_by(ctx, "mp", k) for k in hops], axis=1)
    for n in range(1, len(vocab_jobs)):
        got_vocab.append(fetch(n))

    out_pieces, out_offsets = [], []
    for n, got in enumerate(got_out):
        held = spread(got, "prompt")
        if got.shape[0] % LANES:
            held = [(assemble(held), jnp.int32(0))]
        for piece, owner in held:
            out_pieces.append(piece)
            out_offsets.append(n * w_out.shape[0] + owner * piece.shape[0])
    out_offsets = jnp.stack(out_offsets).astype(jnp.int32)

    vocab_sets = []
    for n, got in enumerate(got_vocab):
        held = spread(got, "prompt")
        first = (ring_source("dp", vocab_jobs[n][0]) * n_model + lax.axis_index("mp")) * w_vocab.shape[1]
        first = first + vocab_jobs[n][1] * part_cols
        scalars = jnp.stack([first] + [o * p.shape[0] for p, o in held]).astype(jnp.int32)
        vocab_sets.append(([p for p, _ in held], scalars))

    def tiled(flat):
        return jnp.tile(flat, (prompts_here,) + (1,) * (flat.ndim - 1))

    own_first = ((my_seq * n_model + lax.axis_index("mp")) * w_vocab.shape[1]).astype(jnp.int32)
    own_scalars = jnp.stack([own_first, jnp.int32(0)])
    sets = []
    rows = out_project(ctx, other_a, tiled(flat_embed), final_gain, w_out, out_pieces, out_offsets)
    ids = tiled(labels.reshape(-1))
    stats = vocab_stats(rows, ids, [w_vocab], own_scalars, fresh_stats(rows.shape[0]))
    sets.append([rows, ids, stats])
    if paired:
        other_b = jnp.concatenate([shift_by(ctx_pair, "mp", k) for k in hops], axis=1)
        embed_pair = assemble(spread(got_embed, "prompt"))
        ids = tiled(swap_pair(labels.reshape(-1), "dp"))
        rows = out_project(ctx_pair, other_b, tiled(embed_pair), final_gain, w_out, out_pieces, out_offsets)
        stats = vocab_stats(rows, ids, [w_vocab], own_scalars, fresh_stats(rows.shape[0]))
        sets.append([rows, ids, stats])
    for pieces, scalars in vocab_sets:
        for entry in sets:
            entry[2] = vocab_stats(entry[0], entry[1], pieces, scalars, entry[2])

    merged = fold_lanes(sets[0][2])
    if paired:
        merged = combine_stats(merged, swap_pair(fold_lanes(sets[1][2]), "dp"))
    for other in [shift_by(merged, "mp", k) for k in hops]:
        merged = combine_stats(merged, other)
    losses = merged[0] + jnp.log(merged[1]) - merged[2]
    losses = losses.reshape(prompts_here, seq_count, target_len)
    valid = jnp.arange(target_len, dtype=jnp.int32)[None, :] < lengths[:, None]
    token_loss = jnp.where(valid[None], losses, 0.0)
    prompt_sums = jnp.sum(token_loss, axis=(1, 2))
    counted = jnp.sum(lengths).astype(jnp.float32)
    sums = jnp.sum(small_gather(jnp.concatenate([prompt_sums, counted[None]]), "dp"), axis=0)
    table = small_gather(sums, "prompt")
    prompt_loss = table[:, :prompts_here].reshape(-1) / table[0, prompts_here]
    return (token_loss, prompt_loss)


def solution(mesh):
    return jax.shard_map(
        shards,
        mesh=mesh,
        in_specs=(
            P("prompt", None, None),
            P("dp", None, None),
            P("dp", None),
            P("dp"),
            P(),
            P(None, None, "mp"),
            P("mp", None),
            P(),
            P(None, ("dp", "mp")),
        ),
        out_specs=(P("prompt", "dp", None), P()),
        check_vma=False,
    )
```

profile of v0, /device:TPU:1, one launch (start us, length us, event | category | flops | bytes accessed | tf_op | source)
XLA Modules:
  0.0 516.3 jit_solution(7736436763505478342)
XLA Ops:
  0.6 1.7 constant_dynamic-slice_fusion.1
  2.4 2.1 collective-permute-start.1
  4.5 3.9 fusion.8
  8.4 2.3 collective-permute-start.5
  10.7 2.3 dynamic-slice_bitcast_fusion
  13.1 1.3 collective-permute-start.23
  14.5 2.4 copy.23
  16.9 1.6 pad.4.clone
  18.5 1.4 fusion
  20.0 1.2 pad_maximum_fusion
  21.2 28.8 %collective-permute-done.1.rest_0_ = bf16[256,4096]{1,0:T(8,128)(2,1)} collective-permute-done((bf16[256,4096]{1,0:T(8,128)(2,1)S(1)}, bf16[256,4096]{1,0:T(8,128)(2,1)}, u32[]{:S(2)}, u32[]{:S(2)}) %collective-permute-start.1) | collective-permute-done | bytes 2097184 | tf_op jit(solution)/shard_map/ppermute | solution.py:21
  49.9 1.2 collective-permute-start.2
  51.1 27.8 %qkv_rope.1.q_ref.k_ref.v_ref = bf16[3,768,1024]{2,1,0:T(8,128)(2,1)} custom-call(bf16[512,4096]{1,0:T(8,128)(2,1)} %bitcast.64, bf16[256,4096]{1,0:T(8,128)(2,1)} %bitcast.66, f32[1,4096]{1,0:T(1,128)} %bitcast.106, bf16[3,4096,1024]{2,1,0:T(8,128)(2,1)} %w_ref.3, f32[768,128]{1,0:T(8,128)} %get-tuple-element.81.cos_ref, f32[768,128]{1,0:T(8,128)} %get-tuple-element.82.sin_ref), custom_call_target="tpu_custom_call" | custom-call | flops 19327352832 | bytes 25165824 | tf_op jit(solution)/shard_map/qkv_rope/pallas_call | solution.py:141
  78.9 2.4 collective-permute-start.13
  81.3 12.4 %attend.1 = bf16[2,512,1024]{2,1,0:T(8,128)(2,1)} custom-call(bf16[3,768,1024]{2,1,0:T(8,128)(2,1)} %qkv_rope.1.q_ref.k_ref.v_ref, bf16[3,768,1024]{2,1,0:T(8,128)(2,1)} %qkv_rope.1.q_ref.k_ref.v_ref, bf16[3,768,1024]{2,1,0:T(8,128)(2,1)} %qkv_rope.1.q_ref.k_ref.v_ref), custom_call_target="tpu_custom_call" | custom-call | flops 2684354560 | bytes 6291456 | tf_op jit(solution)/shard_map/attend/pallas_call | solution.py:206
  93.7 1.2 collective-permute-start
  95.0 28.6 %collective-permute-done.9.rest_0_ = bf16[1024,512]{1,0:T(8,128)(2,1)} collective-permute-done((bf16[1024,512]{1,0:T(8,128)(2,1)}, bf16[1024,512]{1,0:T(8,128)(2,1)}, u32[]{:S(2)}, u32[]{:S(2)}) %collective-permute-start.9) | collective-permute-done | bytes 1048608 | tf_op jit(solution)/shard_map/ppermute | solution.py:21
  123.5 1.2 collective-permute-start.24
  124.8 43.6 %collective-permute-done.13.rest_0_ = bf16[1024,512]{1,0:T(8,128)(2,1)} collective-permute-done((bf16[1024,512]{1,0:T(8,128)(2,1)S(1)}, bf16[1024,512]{1,0:T(8,128)(2,1)}, u32[]{:S(2)}, u32[]{:S(2)}) %collective-permute-start.13) | collective-permute-done | bytes 1048608 | tf_op jit(solution)/shard_map/ppermute | solution.py:21
  168.5 2.6 collective-permute-start.25
  171.7 1.0 copy.25
  176.7 14.3 %collective-permute-done.17.rest_0_ = bf16[1024,512]{1,0:T(8,128)(2,1)} collective-permute-done((bf16[1024,512]{1,0:T(8,128)(2,1)S(1)}, bf16[1024,512]{1,0:T(8,128)(2,1)}, u32[]{:S(2)}, u32[]{:S(2)}) %collective-permute-start.17) | collective-permute-done | bytes 1048608 | tf_op jit(solution)/shard_map/ppermute | solution.py:21
  191.0 1.5 collective-permute-start.3
  193.0 1.0 copy.27
  194.0 2.5 tile.36
  196.5 2.4 constant_dynamic-update-slice_fusion.3
  199.0 1.2 collective-permute-start.6
  200.6 2.3 constant_dynamic-update-slice_fusion.2
  203.2 2.3 constant_dynamic-update-slice_fusion.1
  205.4 2.3 constant_dynamic-update-slice_fusion
  207.8 16.1 %collective-permute-done.6.rest_1_ = bf16[1024,512]{1,0:T(8,128)(2,1)} collective-permute-done((bf16[1024,512]{1,0:T(8,128)(2,1)}, bf16[1024,512]{1,0:T(8,128)(2,1)}, u32[]{:S(2)}, u32[]{:S(2)}) %collective-permute-start.6) | collective-permute-done | bytes 1048608 | tf_op jit(solution)/shard_map/ppermute | solution.py:51
  223.9 1.2 collective-permute-start.10
  225.1 1.2 collective-permute-start.11
  226.6 1.2 collective-permute-start.18
  227.8 4.3 tile.32
  232.2 30.3 %out_project.2.rows_ref = bf16[1024,4096]{1,0:T(8,128)(2,1)} custom-call(s32[4]{0:T(128)} %pad_add_fusion.owners_ref, bf16[1024,1024]{1,0:T(8,128)(2,1)} %bitcast.68, bf16[1024,1024]{1,0:T(8,128)(2,1)} %collective-permute-done.other_ref, bf16[1024,4096]{1,0:T(8,128)(2,1)} %bitcast.63, f32[1,4096]{1,0:T(1,128)} %bitcast.107, bf16[1024,4096]{1,0:T(8,128)(2,1)} %w_ref.5, ...), custom_call_target="tpu_custom_call" | custom-call | flops 17179869184 | bytes 16777216 | tf_op jit(solution)/shard_map/out_project/pallas_call | solution.py:268
  263.3 7.2 %collective-permute-done.14.rest_1_ = bf16[1024,512]{1,0:T(8,128)(2,1)} collective-permute-done((bf16[1024,512]{1,0:T(8,128)(2,1)}, bf16[1024,512]{1,0:T(8,128)(2,1)}, u32[]{:S(2)}, u32[]{:S(2)}) %collective-permute-start.14) | collective-permute-done | bytes 1048608 | tf_op jit(solution)/shard_map/ppermute | solution.py:51
  270.5 3.2 collective-permute-start.12
  273.7 19.3 %collective-permute-done.18.rest_1_ = bf16[1024,512]{1,0:T(8,128)(2,1)} collective-permute-done((bf16[1024,512]{1,0:T(8,128)(2,1)}, bf16[1024,512]{1,0:T(8,128)(2,1)}, u32[]{:S(2)}, u32[]{:S(2)}) %collective-permute-start.18) | collective-permute-done | bytes 1048608 | tf_op jit(solution)/shard_map/ppermute | solution.py:51
  293.0 1.8 collective-permute-start.16
  296.6 28.2 %vocab_stats.10 = (f32[1024,128]{1,0:T(8,128)}, f32[1024,128]{1,0:T(8,128)}, f32[1024,128]{1,0:T(8,128)}) custom-call(s32[2]{0:T(128)} %pad_add_fusion.1.scalars_ref, bf16[1024,4096]{1,0:T(8,128)(2,1)} %out_project.2.rows_ref, s32[1024,1]{1,0:T(8,128)} %bitcast.75, f32[1024,128]{1,0:T(8,128)} %broadcast_14_top_in.2.top_in, ...), custom_call_target="tpu_custom_call" | custom-call | flops 17179869184 | bytes 16777216 | tf_op jit(solution)/shard_map/vocab_stats/pallas_call | solution.py:345
  325.4 11.8 %vocab_stats.11 = (f32[1024,128]{1,0:T(8,128)}, f32[1024,128]{1,0:T(8,128)}, f32[1024,128]{1,0:T(8,128)}) custom-call(s32[5]{0:T(128)} %stack.133.scalars_ref, bf16[1024,4096]{1,0:T(8,128)(2,1)} %out_project.2.rows_ref, s32[1024,1]{1,0:T(8,128)} %bitcast.76, f32[1024,128]{1,0:T(8,128)} %get-tuple-element.33.top_in, f32[1024,128]{1,0:T(8,128)} %get-tuple-element.34.mass_in, ...), custom_call_target="tpu_custom_call" | custom-call | flops 4294967296 | bytes 4194304 | tf_op jit(solution)/shard_map/vocab_stats/pallas_call | solution.py:345
  337.2 11.8 %vocab_stats.12 = (f32[1024,128]{1,0:T(8,128)}, f32[1024,128]{1,0:T(8,128)}, f32[1024,128]{1,0:T(8,128)}) custom-call(s32[5]{0:T(128)} %stack.131.scalars_ref, bf16[1024,4096]{1,0:T(8,128)(2,1)} %out_project.2.rows_ref, s32[1024,1]{1,0:T(8,128)} %bitcast.77, f32[1024,128]{1,0:T(8,128)} %get-tuple-element.36.top_in, f32[1024,128]{1,0:T(8,128)} %get-tuple-element.37.mass_in, ...), custom_call_target="tpu_custom_call" | custom-call | flops 4294967296 | bytes 4194304 | tf_op jit(solution)/shard_map/vocab_stats/pallas_call | solution.py:345
  349.1 11.9 %vocab_stats.13 = (f32[1024,128]{1,0:T(8,128)}, f32[1024,128]{1,0:T(8,128)}, f32[1024,128]{1,0:T(8,128)}) custom-call(s32[5]{0:T(128)} %stack.129.scalars_ref, bf16[1024,4096]{1,0:T(8,128)(2,1)} %out_project.2.rows_ref, s32[1024,1]{1,0:T(8,128)} %bitcast.78, f32[1024,128]{1,0:T(8,128)} %get-tuple-element.39.top_in, f32[1024,128]{1,0:T(8,128)} %get-tuple-element.40.mass_in, ...), custom_call_target="tpu_custom_call" | custom-call | flops 4294967296 | bytes 4194304 | tf_op jit(solution)/shard_map/vocab_stats/pallas_call | solution.py:345
  361.0 0.9 copy-done.7
  362.3 12.0 %vocab_stats.14 = (f32[1024,128]{1,0:T(8,128)}, f32[1024,128]{1,0:T(8,128)}, f32[1024,128]{1,0:T(8,128)}) custom-call(s32[5]{0:T(128)} %stack.122.scalars_ref, bf16[1024,4096]{1,0:T(8,128)(2,1)} %out_project.2.rows_ref, s32[1024,1]{1,0:T(8,128)} %bitcast.79, f32[1024,128]{1,0:T(8,128)} %get-tuple-element.42.top_in, f32[1024,128]{1,0:T(8,128)} %get-tuple-element.43.mass_in, ...), custom_call_target="tpu_custom_call" | custom-call | flops 4294967296 | bytes 4194304 | tf_op jit(solution)/shard_map/vocab_stats/pallas_call | solution.py:345
  374.2 1.2 reduce_max.22
  375.5 6.5 %tile.37 = bf16[2,512,4096]{2,1,0:T(8,128)(2,1)} broadcast(bf16[512,4096]{1,0:T(8,128)(2,1)} %constant_dynamic-update-slice_fusion), dimensions={1,2} | broadcast | bytes 12582912 | tf_op jit(solution)/shard_map/tile | solution.py:449
  382.0 30.1 %out_project.3.rows_ref = bf16[1024,4096]{1,0:T(8,128)(2,1)} custom-call(s32[4]{0:T(128)} %pad_add_fusion.owners_ref, bf16[1024,1024]{1,0:T(8,128)(2,1)} %collective-permute-done.21.ctx_ref, bf16[1024,1024]{1,0:T(8,128)(2,1)} %collective-permute-done.22.other_ref, bf16[1024,4096]{1,0:T(8,128)(2,1)} %bitcast.62, f32[1,4096]{1,0:T(1,128)} %bitcast.108, ...), custom_call_target="tpu_custom_call" | custom-call | flops 17179869184 | bytes 16777216 | tf_op jit(solution)/shard_map/out_project/pallas_call | solution.py:268
  412.1 28.0 %vocab_stats.15 = (f32[1024,128]{1,0:T(8,128)}, f32[1024,128]{1,0:T(8,128)}, f32[1024,128]{1,0:T(8,128)}) custom-call(s32[2]{0:T(128)} %pad_add_fusion.1.scalars_ref, bf16[1024,4096]{1,0:T(8,128)(2,1)} %out_project.3.rows_ref, s32[1024,1]{1,0:T(8,128)} %bitcast.70, f32[1024,128]{1,0:T(8,128)} %broadcast_14_top_in.2.top_in, ...), custom_call_target="tpu_custom_call" | custom-call | flops 17179869184 | bytes 16777216 | tf_op jit(solution)/shard_map/vocab_stats/pallas_call | solution.py:345
  440.1 11.9 %vocab_stats.16 = (f32[1024,128]{1,0:T(8,128)}, f32[1024,128]{1,0:T(8,128)}, f32[1024,128]{1,0:T(8,128)}) custom-call(s32[5]{0:T(128)} %stack.133.scalars_ref, bf16[1024,4096]{1,0:T(8,128)(2,1)} %out_project.3.rows_ref, s32[1024,1]{1,0:T(8,128)} %bitcast.71, f32[1024,128]{1,0:T(8,128)} %get-tuple-element.46.top_in, f32[1024,128]{1,0:T(8,128)} %get-tuple-element.47.mass_in, ...), custom_call_target="tpu_custom_call" | custom-call | flops 4294967296 | bytes 4194304 | tf_op jit(solution)/shard_map/vocab_stats/pallas_call | solution.py:345
  452.1 11.9 %vocab_stats.17 = (f32[1024,128]{1,0:T(8,128)}, f32[1024,128]{1,0:T(8,128)}, f32[1024,128]{1,0:T(8,128)}) custom-call(s32[5]{0:T(128)} %stack.131.scalars_ref, bf16[1024,4096]{1,0:T(8,128)(2,1)} %out_project.3.rows_ref, s32[1024,1]{1,0:T(8,128)} %bitcast.72, f32[1024,128]{1,0:T(8,128)} %get-tuple-element.49.top_in, f32[1024,128]{1,0:T(8,128)} %get-tuple-element.50.mass_in, ...), custom_call_target="tpu_custom_call" | custom-call | flops 4294967296 | bytes 4194304 | tf_op jit(solution)/shard_map/vocab_stats/pallas_call | solution.py:345
  463.9 11.8 %vocab_stats.18 = (f32[1024,128]{1,0:T(8,128)}, f32[1024,128]{1,0:T(8,128)}, f32[1024,128]{1,0:T(8,128)}) custom-call(s32[5]{0:T(128)} %stack.129.scalars_ref, bf16[1024,4096]{1,0:T(8,128)(2,1)} %out_project.3.rows_ref, s32[1024,1]{1,0:T(8,128)} %bitcast.73, f32[1024,128]{1,0:T(8,128)} %get-tuple-element.52.top_in, f32[1024,128]{1,0:T(8,128)} %get-tuple-element.53.mass_in, ...), custom_call_target="tpu_custom_call" | custom-call | flops 4294967296 | bytes 4194304 | tf_op jit(solution)/shard_map/vocab_stats/pallas_call | solution.py:345
  475.8 12.3 %vocab_stats.19 = (f32[1024,128]{1,0:T(8,128)}, f32[1024,128]{1,0:T(8,128)}, f32[1024,128]{1,0:T(8,128)}) custom-call(s32[5]{0:T(128)} %stack.122.scalars_ref, bf16[1024,4096]{1,0:T(8,128)(2,1)} %out_project.3.rows_ref, s32[1024,1]{1,0:T(8,128)} %bitcast.74, f32[1024,128]{1,0:T(8,128)} %get-tuple-element.55.top_in, f32[1024,128]{1,0:T(8,128)} %get-tuple-element.56.mass_in, ...), custom_call_target="tpu_custom_call" | custom-call | flops 4294967296 | bytes 4194304 | tf_op jit(solution)/shard_map/vocab_stats/pallas_call | solution.py:345
  488.1 1.2 reduce_max.24
  489.3 1.2 reduce_sum.67
  490.6 1.6 multiply_reduce_fusion.1
  493.2 1.6 collective-permute-done.28
  494.9 1.4 collective-permute-start.29
  496.3 1.3 collective-permute-done.29
  498.6 3.2 collective-permute-start.31
  502.8 1.4 collective-permute-done.32
  504.9 5.4 %collective-permute-start.33 = (f32[3]{0:T(128)S(1)}, f32[3]{0:T(128)S(1)}, u32[]{:S(2)}, u32[]{:S(2)}) collective-permute-start(f32[3]{0:T(128)S(1)} %select_reduce_fusion), channel_id=1, source_target_pairs={{0,8},{8,16},{16,24},{24,0},{1,9},{9,17},{17,25},{25,1},{2,10},{10... | collective-permute-start | bytes 44 | tf_op jit(solution)/shard_map/ppermute | solution.py:21
  511.0 1.7 collective-permute-done.34
  (101 shorter events, 17.0 us)
Async XLA Ops:
  2.4 47.6 %collective-permute-start.1 = (bf16[256,4096]{1,0:T(8,128)(2,1)S(1)}, bf16[256,4096]{1,0:T(8,128)(2,1)}, u32[]{:S(2)}, u32[]{:S(2)}) collective-permute-start(bf16[256,4096]{1,0:T(8,128)(2,1)S(1)} %constant_dynamic-slice_fusion.1), channel_id=1, source_target_pairs={{0,1},{1,0},{2,3},{3,2},{4,5},{5,4},{6,7},{7,6},{8,9},{9,8},{10,11... | collective-permute-start | bytes 6291464 | tf_op jit(solution)/shard_map/ppermute | solution.py:21
  4.5 9.9 %copy-start.6 = (s32[1,512]{1,0:T(1,128)S(1)}, s32[1,512]{1,0:T(1,128)}, u32[]{:S(2)}) copy-start(s32[1,512]{1,0:T(1,128)} %param.13) | copy-start | bytes 6148
  8.4 85.3 %collective-permute-start.5 = (bf16[1024,512]{1,0:T(8,128)(2,1)}, bf16[1024,512]{1,0:T(8,128)(2,1)}, u32[]{:S(2)}, u32[]{:S(2)}) collective-permute-start(bf16[1024,512]{1,0:T(8,128)(2,1)} %get-tuple-element.68), channel_id=1, source_target_pairs={{0,4},{2,6},{4,0},{6,2},{1,5},{3,7},{5,1},{7,3},{8,12},{10,14},{12... | collective-permute-start | bytes 3145736 | tf_op jit(solution)/shard_map/ppermute | solution.py:21
  10.7 112.9 %collective-permute-start.9 = (bf16[1024,512]{1,0:T(8,128)(2,1)}, bf16[1024,512]{1,0:T(8,128)(2,1)}, u32[]{:S(2)}, u32[]{:S(2)}) collective-permute-start(bf16[1024,512]{1,0:T(8,128)(2,1)} %get-tuple-element.67), channel_id=1, source_target_pairs={{0,4},{2,6},{4,0},{6,2},{1,5},{3,7},{5,1},{7,3},{8,12},{10,14},{12... | collective-permute-start | bytes 3145736 | tf_op jit(solution)/shard_map/ppermute | solution.py:21
  13.1 110.5 %collective-permute-start.23 = (bf16[128,4096]{1,0:T(8,128)(2,1)}, bf16[128,4096]{1,0:T(8,128)(2,1)}, u32[]{:S(2)}, u32[]{:S(2)}) collective-permute-start(bf16[128,4096]{1,0:T(8,128)(2,1)} %dynamic-slice_bitcast_fusion), channel_id=1, source_target_pairs={{0,2},{2,0},{4,6},{6,4},{1,3},{3,1},{5,7},{7,5},{8,10},{10,8},{12,... | collective-permute-start | bytes 3145736 | tf_op jit(solution)/shard_map/ppermute | solution.py:382
  14.4 64.5 %collective-permute-start.27 = (s32[512]{0:T(512)S(1)}, s32[512]{0:T(512)S(1)}, u32[]{:S(2)}, u32[]{:S(2)}) collective-permute-start(s32[512]{0:T(512)S(1)} %bitcast.97), channel_id=1, source_target_pairs={{0,2},{2,0},{4,6},{6,4},{1,3},{3,1},{5,7},{7,5},{8,10},{10,8},{12,... | collective-permute-start | bytes 6152 | tf_op jit(solution)/shard_map/ppermute | solution.py:382
  49.9 142.5 %collective-permute-start.2 = (bf16[256,4096]{1,0:T(8,128)(2,1)}, bf16[256,4096]{1,0:T(8,128)(2,1)}, u32[]{:S(2)}, u32[]{:S(2)}) collective-permute-start(bf16[256,4096]{1,0:T(8,128)(2,1)} %collective-permute-done.1.rest_0_), channel_id=1, source_target_pairs={{0,16},{8,24},{16,0},{24,8},{1,17},{9,25},{17,1},{25,9},{2,18},{10... | collective-permute-start | bytes 6291464 | tf_op jit(solution)/shard_map/ppermute | solution.py:51
  51.1 27.8 %copy-start.3 = (bf16[1024,512]{1,0:T(8,128)(2,1)S(1)}, bf16[1024,512]{1,0:T(8,128)(2,1)}, u32[]{:S(2)}) copy-start(bf16[1024,512]{1,0:T(8,128)(2,1)} %get-tuple-element.66) | copy-start | bytes 3145732
  78.9 89.6 %collective-permute-start.13 = (bf16[1024,512]{1,0:T(8,128)(2,1)S(1)}, bf16[1024,512]{1,0:T(8,128)(2,1)}, u32[]{:S(2)}, u32[]{:S(2)}) collective-permute-start(bf16[1024,512]{1,0:T(8,128)(2,1)S(1)} %copy-done.3), channel_id=1, source_target_pairs={{0,4},{2,6},{4,0},{6,2},{1,5},{3,7},{5,1},{7,3},{8,12},{10,14},{12... | collective-permute-start | bytes 3145736 | tf_op jit(solution)/shard_map/ppermute | solution.py:21
  93.7 105.2 %collective-permute-start = (bf16[1024,1024]{1,0:T(8,128)(2,1)}, bf16[1024,1024]{1,0:T(8,128)(2,1)}, u32[]{:S(2)}, u32[]{:S(2)}) collective-permute-start(bf16[1024,1024]{1,0:T(8,128)(2,1)} %bitcast.67), channel_id=1, source_target_pairs={{0,1},{1,0},{2,3},{3,2},{4,5},{5,4},{6,7},{7,6},{8,9},{9,8},{10,11... | collective-permute-start | bytes 6291464 | tf_op jit(solution)/shard_map/ppermute | solution.py:21
  123.5 67.4 %collective-permute-start.17 = (bf16[1024,512]{1,0:T(8,128)(2,1)S(1)}, bf16[1024,512]{1,0:T(8,128)(2,1)}, u32[]{:S(2)}, u32[]{:S(2)}) collective-permute-start(bf16[1024,512]{1,0:T(8,128)(2,1)S(1)} %get-tuple-element.65), channel_id=1, source_target_pairs={{0,4},{2,6},{4,0},{6,2},{1,5},{3,7},{5,1},{7,3},{8,12},{10,14},{12... | collective-permute-start | bytes 3145736 | tf_op jit(solution)/shard_map/ppermute | solution.py:21
  123.5 68.9 %collective-permute-start.24 = (bf16[128,4096]{1,0:T(8,128)(2,1)}, bf16[128,4096]{1,0:T(8,128)(2,1)}, u32[]{:S(2)}, u32[]{:S(2)}) collective-permute-start(bf16[128,4096]{1,0:T(8,128)(2,1)} %collective-permute-done.23), channel_id=1, source_target_pairs={{0,16},{8,24},{16,0},{24,8},{1,17},{9,25},{17,1},{25,9},{2,18},{10... | collective-permute-start | bytes 3145736 | tf_op jit(solution)/shard_map/ppermute | solution.py:51
  168.5 31.7 %collective-permute-start.25 = (bf16[128,4096]{1,0:T(8,128)(2,1)}, bf16[128,4096]{1,0:T(8,128)(2,1)}, u32[]{:S(2)}, u32[]{:S(2)}) collective-permute-start(bf16[128,4096]{1,0:T(8,128)(2,1)} %collective-permute-done.23), channel_id=1, source_target_pairs={{0,8},{8,0},{16,24},{24,16},{1,9},{9,1},{17,25},{25,17},{2,10},{10... | collective-permute-start | bytes 3145736 | tf_op jit(solution)/shard_map/ppermute | solution.py:51
  191.0 35.4 %collective-permute-start.3 = (bf16[256,4096]{1,0:T(8,128)(2,1)}, bf16[256,4096]{1,0:T(8,128)(2,1)}, u32[]{:S(2)}, u32[]{:S(2)}) collective-permute-start(bf16[256,4096]{1,0:T(8,128)(2,1)} %collective-permute-done.1.rest_0_), channel_id=1, source_target_pairs={{0,8},{8,0},{16,24},{24,16},{1,9},{9,1},{17,25},{25,17},{2,10},{10... | collective-permute-start | bytes 6291464 | tf_op jit(solution)/shard_map/ppermute | solution.py:51
  192.5 10.4 %collective-permute-start.26 = (bf16[128,4096]{1,0:T(8,128)(2,1)}, bf16[128,4096]{1,0:T(8,128)(2,1)}, u32[]{:S(2)}, u32[]{:S(2)}) collective-permute-start(bf16[128,4096]{1,0:T(8,128)(2,1)} %collective-permute-done.24), channel_id=1, source_target_pairs={{0,8},{8,0},{16,24},{24,16},{1,9},{9,1},{17,25},{25,17},{2,10},{10... | collective-permute-start | bytes 3145736 | tf_op jit(solution)/shard_map/ppermute | solution.py:51
  192.5 34.1 %collective-permute-start.4 = (bf16[256,4096]{1,0:T(8,128)(2,1)}, bf16[256,4096]{1,0:T(8,128)(2,1)}, u32[]{:S(2)}, u32[]{:S(2)}) collective-permute-start(bf16[256,4096]{1,0:T(8,128)(2,1)} %collective-permute-done.2.rest_1_), channel_id=1, source_target_pairs={{0,8},{8,0},{16,24},{24,16},{1,9},{9,1},{17,25},{25,17},{2,10},{10... | collective-permute-start | bytes 6291464 | tf_op jit(solution)/shard_map/ppermute | solution.py:51
  194.0 8.8 %copy-start.2 = (bf16[2,512,1024]{2,1,0:T(8,128)(2,1)S(1)}, bf16[2,512,1024]{2,1,0:T(8,128)(2,1)}, u32[]{:S(2)}) copy-start(bf16[2,512,1024]{2,1,0:T(8,128)(2,1)} %attend.1) | copy-start | bytes 6291460
  196.5 31.3 %copy-start = (bf16[1,512,4096]{2,1,0:T(8,128)(2,1)S(1)}, bf16[1,512,4096]{2,1,0:T(8,128)(2,1)}, u32[]{:S(2)}) copy-start(bf16[1,512,4096]{2,1,0:T(8,128)(2,1)} %param.12) | copy-start | bytes 12582916
  199.0 25.0 %collective-permute-start.6 = (bf16[1024,512]{1,0:T(8,128)(2,1)}, bf16[1024,512]{1,0:T(8,128)(2,1)}, u32[]{:S(2)}, u32[]{:S(2)}) collective-permute-start(bf16[1024,512]{1,0:T(8,128)(2,1)} %collective-permute-done.5.rest_0_), channel_id=1, source_target_pairs={{0,16},{8,24},{16,0},{24,8},{1,17},{9,25},{17,1},{25,9},{2,18},{10... | collective-permute-start | bytes 3145736 | tf_op jit(solution)/shard_map/ppermute | solution.py:51
  200.2 24.9 %collective-permute-start.7 = (bf16[1024,512]{1,0:T(8,128)(2,1)}, bf16[1024,512]{1,0:T(8,128)(2,1)}, u32[]{:S(2)}, u32[]{:S(2)}) collective-permute-start(bf16[1024,512]{1,0:T(8,128)(2,1)} %collective-permute-done.5.rest_0_), channel_id=1, source_target_pairs={{0,8},{8,0},{16,24},{24,16},{1,9},{9,1},{17,25},{25,17},{2,10},{10... | collective-permute-start | bytes 3145736 | tf_op jit(solution)/shard_map/ppermute | solution.py:51
  202.9 91.9 %collective-permute-start.21 = (bf16[1024,1024]{1,0:T(8,128)(2,1)S(1)}, bf16[1024,1024]{1,0:T(8,128)(2,1)}, u32[]{:S(2)}, u32[]{:S(2)}) collective-permute-start(bf16[1024,1024]{1,0:T(8,128)(2,1)S(1)} %bitcast.69), channel_id=1, source_target_pairs={{0,2},{2,0},{4,6},{6,4},{1,3},{3,1},{5,7},{7,5},{8,10},{10,8},{12,... | collective-permute-start | bytes 6291464 | tf_op jit(solution)/shard_map/ppermute | solution.py:382
  223.9 38.6 %collective-permute-start.10 = (bf16[1024,512]{1,0:T(8,128)(2,1)}, bf16[1024,512]{1,0:T(8,128)(2,1)}, u32[]{:S(2)}, u32[]{:S(2)}) collective-permute-start(bf16[1024,512]{1,0:T(8,128)(2,1)} %collective-permute-done.9.rest_0_), channel_id=1, source_target_pairs={{0,16},{8,24},{16,0},{24,8},{1,17},{9,25},{17,1},{25,9},{2,18},{10... | collective-permute-start | bytes 3145736 | tf_op jit(solution)/shard_map/ppermute | solution.py:51
  225.1 38.1 %collective-permute-start.11 = (bf16[1024,512]{1,0:T(8,128)(2,1)}, bf16[1024,512]{1,0:T(8,128)(2,1)}, u32[]{:S(2)}, u32[]{:S(2)}) collective-permute-start(bf16[1024,512]{1,0:T(8,128)(2,1)} %collective-permute-done.9.rest_0_), channel_id=1, source_target_pairs={{0,8},{8,0},{16,24},{24,16},{1,9},{9,1},{17,25},{25,17},{2,10},{10... | collective-permute-start | bytes 3145736 | tf_op jit(solution)/shard_map/ppermute | solution.py:51
  226.4 44.1 %collective-permute-start.14 = (bf16[1024,512]{1,0:T(8,128)(2,1)}, bf16[1024,512]{1,0:T(8,128)(2,1)}, u32[]{:S(2)}, u32[]{:S(2)}) collective-permute-start(bf16[1024,512]{1,0:T(8,128)(2,1)} %collective-permute-done.13.rest_0_), channel_id=1, source_target_pairs={{0,16},{8,24},{16,0},{24,8},{1,17},{9,25},{17,1},{25,9},{2,18},{10... | collective-permute-start | bytes 3145736 | tf_op jit(solution)/shard_map/ppermute | solution.py:51
  226.6 66.4 %collective-permute-start.18 = (bf16[1024,512]{1,0:T(8,128)(2,1)}, bf16[1024,512]{1,0:T(8,128)(2,1)}, u32[]{:S(2)}, u32[]{:S(2)}) collective-permute-start(bf16[1024,512]{1,0:T(8,128)(2,1)} %collective-permute-done.17.rest_0_), channel_id=1, source_target_pairs={{0,16},{8,24},{16,0},{24,8},{1,17},{9,25},{17,1},{25,9},{2,18},{10... | collective-permute-start | bytes 3145736 | tf_op jit(solution)/shard_map/ppermute | solution.py:51
  262.5 86.6 %collective-permute-start.15 = (bf16[1024,512]{1,0:T(8,128)(2,1)}, bf16[1024,512]{1,0:T(8,128)(2,1)}, u32[]{:S(2)}, u32[]{:S(2)}) collective-permute-start(bf16[1024,512]{1,0:T(8,128)(2,1)} %collective-permute-done.13.rest_0_), channel_id=1, source_target_pairs={{0,8},{8,0},{16,24},{24,16},{1,9},{9,1},{17,25},{25,17},{2,10},{10... | collective-permute-start | bytes 3145736 | tf_op jit(solution)/shard_map/ppermute | solution.py:51
  263.2 61.6 %collective-permute-start.8 = (bf16[1024,512]{1,0:T(8,128)(2,1)}, bf16[1024,512]{1,0:T(8,128)(2,1)}, u32[]{:S(2)}, u32[]{:S(2)}) collective-permute-start(bf16[1024,512]{1,0:T(8,128)(2,1)} %collective-permute-done.6.rest_1_), channel_id=1, source_target_pairs={{0,8},{8,0},{16,24},{24,16},{1,9},{9,1},{17,25},{25,17},{2,10},{10... | collective-permute-start | bytes 3145736 | tf_op jit(solution)/shard_map/ppermute | solution.py:51
  270.5 54.7 %collective-permute-start.12 = (bf16[1024,512]{1,0:T(8,128)(2,1)}, bf16[1024,512]{1,0:T(8,128)(2,1)}, u32[]{:S(2)}, u32[]{:S(2)}) collective-permute-start(bf16[1024,512]{1,0:T(8,128)(2,1)} %collective-permute-done.10.rest_1_), channel_id=1, source_target_pairs={{0,8},{8,0},{16,24},{24,16},{1,9},{9,1},{17,25},{25,17},{2,10},{10... | collective-permute-start | bytes 3145736 | tf_op jit(solution)/shard_map/ppermute | solution.py:51
  293.0 56.1 %collective-permute-start.16 = (bf16[1024,512]{1,0:T(8,128)(2,1)}, bf16[1024,512]{1,0:T(8,128)(2,1)}, u32[]{:S(2)}, u32[]{:S(2)}) collective-permute-start(bf16[1024,512]{1,0:T(8,128)(2,1)} %collective-permute-done.14.rest_1_), channel_id=1, source_target_pairs={{0,8},{8,0},{16,24},{24,16},{1,9},{9,1},{17,25},{25,17},{2,10},{10... | collective-permute-start | bytes 3145736 | tf_op jit(solution)/shard_map/ppermute | solution.py:51
  294.7 80.8 %collective-permute-start.22 = (bf16[1024,1024]{1,0:T(8,128)(2,1)}, bf16[1024,1024]{1,0:T(8,128)(2,1)}, u32[]{:S(2)}, u32[]{:S(2)}) collective-permute-start(bf16[1024,1024]{1,0:T(8,128)(2,1)} %collective-permute-done.21.ctx_ref), channel_id=1, source_target_pairs={{0,1},{1,0},{2,3},{3,2},{4,5},{5,4},{6,7},{7,6},{8,9},{9,8},{10,11... | collective-permute-start | bytes 6291464 | tf_op jit(solution)/shard_map/ppermute | solution.py:21
  324.8 36.1 %collective-permute-start.19 = (bf16[1024,512]{1,0:T(8,128)(2,1)}, bf16[1024,512]{1,0:T(8,128)(2,1)S(1)}, u32[]{:S(2)}, u32[]{:S(2)}) collective-permute-start(bf16[1024,512]{1,0:T(8,128)(2,1)} %collective-permute-done.17.rest_0_), channel_id=1, source_target_pairs={{0,8},{8,0},{16,24},{24,16},{1,9},{9,1},{17,25},{25,17},{2,10},{10... | collective-permute-start | bytes 3145736 | tf_op jit(solution)/shard_map/ppermute | solution.py:51
  325.2 35.8 %collective-permute-start.20 = (bf16[1024,512]{1,0:T(8,128)(2,1)}, bf16[1024,512]{1,0:T(8,128)(2,1)S(1)}, u32[]{:S(2)}, u32[]{:S(2)}) collective-permute-start(bf16[1024,512]{1,0:T(8,128)(2,1)} %collective-permute-done.18.rest_1_), channel_id=1, source_target_pairs={{0,8},{8,0},{16,24},{24,16},{1,9},{9,1},{17,25},{25,17},{2,10},{10... | collective-permute-start | bytes 3145736 | tf_op jit(solution)/shard_map/ppermute | solution.py:51
  360.9 1.0 copy-start.7
  361.0 1.3 copy-start.8
  475.8 16.8 %copy-start.1 = (f32[1024,128]{1,0:T(8,128)S(1)}, f32[1024,128]{1,0:T(8,128)}, u32[]{:S(2)}) copy-start(f32[1024,128]{1,0:T(8,128)} %get-tuple-element.45) | copy-start | bytes 1572868
  475.8 16.8 %copy-start.5 = (f32[1024,128]{1,0:T(8,128)S(1)}, f32[1024,128]{1,0:T(8,128)}, u32[]{:S(2)}) copy-start(f32[1024,128]{1,0:T(8,128)} %get-tuple-element.61) | copy-start | bytes 1572868
  475.8 17.2 %copy-start.4 = (f32[1024,128]{1,0:T(8,128)S(1)}, f32[1024,128]{1,0:T(8,128)}, u32[]{:S(2)}) copy-start(f32[1024,128]{1,0:T(8,128)} %get-tuple-element.62) | copy-start | bytes 1572868
  492.2 2.7 collective-permute-start.28
  494.9 2.7 collective-permute-start.29
  498.3 4.5 collective-permute-start.30
  498.6 4.2 collective-permute-start.31
  501.8 2.4 collective-permute-start.32
  504.9 6.1 %collective-permute-start.33 = (f32[3]{0:T(128)S(1)}, f32[3]{0:T(128)S(1)}, u32[]{:S(2)}, u32[]{:S(2)}) collective-permute-start(f32[3]{0:T(128)S(1)} %select_reduce_fusion), channel_id=1, source_target_pairs={{0,8},{8,16},{16,24},{24,0},{1,9},{9,17},{17,25},{25,1},{2,10},{10... | collective-permute-start | bytes 44 | tf_op jit(solution)/shard_map/ppermute | solution.py:21
  510.3 2.4 collective-permute-start.34
  510.6 3.0 collective-permute-start.35
where the time goes:
time: 520 us; the launch traced here: 516 us
  Pallas kernels  252 us (48%)
  waiting for transfers between devices  165 us (32%)
  local copies, waits for them, and re-layouts  44.6 us (9%)
  starting transfers between devices  40.9 us (8%)
  other arithmetic  11.5 us (2%)
    pallas_call x10, Pallas kernels, vocab_stats(): pl.pallas_call(functools.partial(vocab_body, len(pieces)), grid_spec=pltp...  152 us
    ppermute x14, waiting for transfers between devices, shift_by(): lax.ppermute(value, axis, [(i, (i + hop) % size) for i in range(size)])  121 us
    pallas_call x2, Pallas kernels, out_project(): pl.pallas_call(functools.partial(out_body, len(pieces)), grid_spec=pltpu....  60.4 us
    ppermute x18, waiting for transfers between devices, spread(): lax.ppermute(part, axis, pairs)  42.7 us
    pallas_call x1, Pallas kernels, project(): pl.pallas_call(functools.partial(qkv_body, rows_target), grid=(3, width /...  27.8 us
    ppermute x14, starting transfers between devices, shift_by(): lax.ppermute(value, axis, [(i, (i + hop) % size) for i in range(size)])  19.9 us
    ppermute x18, starting transfers between devices, spread(): lax.ppermute(part, axis, pairs)  18.8 us
    another operation x3, local copies, waits for them, and re-layouts, tiled(): return jnp.tile(flat, (prompts_here,) + (1,) * (flat.ndim - 1))  13.3 us
  transfers between devices with their start and end apart: 36, of which 13 were waited for; matrix products, arithmetic and copies ran while one was open for 7% of the time, Pallas kernels for 28%

commit v1 on v0

--- a/solution.py
+++ b/solution.py
@@ -89,19 +89,28 @@
 
     @pl.when((which == 0) & (pl.program_id(1) == 0))
     def _():
-        for ref, start in ((target_ref, 0), (prompt_ref, rows_target)):
-            step = 64
-
-            def one(i, carry, ref=ref, start=start):
-                lo = pl.multiple_of(i * step, step)
-                wide = ref[pl.ds(lo, step), :].astype(jnp.float32)
-                scale = lax.rsqrt(jnp.mean(wide * wide, axis=-1, keepdims=True) + EPSILON)
-                normed[pl.ds(pl.multiple_of(start + lo, step), step), :] = (
-                    wide * scale * gain_ref[...]
-                ).astype(jnp.bfloat16)
-                return carry
-
-            lax.fori_loop(0, ref.shape[0] // step, one, 0)
+        def normal(raw):
+            wide = raw.astype(jnp.float32)
+            scale = lax.rsqrt(jnp.mean(wide * wide, axis=-1, keepdims=True) + EPSILON)
+            return (wide * scale * gain_ref[...]).astype(jnp.bfloat16)
+
+        step = 64
+
+        def one(i, carry):
+            at = pl.ds(pl.multiple_of(i * step, step), step)
+            normed[at, :] = normal(target_ref[at, :])
+            return carry
+
+        lax.fori_loop(0, rows_target // step, one, 0)
+        count, length, depth = prompt_ref.shape
+        span = (normed.shape[0] - rows_target) // count
+        for p in range(count):
+            base = rows_target + p * span
+            for lo in range(0, length, step):
+                high = min(length, lo + step)
+                normed[base + lo : base + high, :] = normal(prompt_ref[p, lo:high, :])
+            if span > length:
+                normed[base + length : base + span, :] = jnp.zeros((span - length, depth), jnp.bfloat16)
 
     total = normed.shape[0]
     block = 256
@@ -133,9 +142,9 @@
             rows(lo, False)
 
 
-def project(target_rows, prompt_rows, gain, w_qkv, cosine, sine):
+def project(target_rows, prompts, pad_len, gain, w_qkv, cosine, sine):
     rows_target, depth = target_rows.shape
-    total = rows_target + prompt_rows.shape[0]
+    total = rows_target + prompts.shape[0] * pad_len
     width = w_qkv.shape[2]
     tile = largest_tile(width, 512)
     return pl.pallas_call(
@@ -143,7 +152,7 @@
         grid=(3, width // tile),
         in_specs=[
             pl.BlockSpec((rows_target, depth), lambda c, j: (0, 0)),
-            pl.BlockSpec(prompt_rows.shape, lambda c, j: (0, 0)),
+            pl.BlockSpec(prompts.shape, lambda c, j: (0, 0, 0)),
             pl.BlockSpec((1, depth), lambda c, j: (0, 0)),
             pl.BlockSpec((1, depth, tile), lambda c, j: (c, 0, j)),
             pl.BlockSpec((total, HD), lambda c, j: (0, 0)),
@@ -156,7 +165,7 @@
             flops=6 * total * depth * width, bytes_accessed=6 * depth * width, transcendentals=0
         ),
         name="qkv_rope",
-    )(target_rows, prompt_rows, gain.reshape(1, -1), w_qkv, cosine, sine)
+    )(target_rows, prompts, gain.reshape(1, -1), w_qkv, cosine, sine)
 
 
 def attend_body(prompts_here, target_len, seqs, prompt_len, pad_len, q_ref, k_ref, v_ref, out_ref):
@@ -218,151 +227,169 @@
     )(qkv, qkv, qkv)
 
 
-def out_body(piece_count, owners_ref, ctx_ref, other_ref, embed_ref, gain_ref, w_ref, *rest):
-    piece_refs = rest[:piece_count]
-    out_ref, hidden, squares, turned = rest[piece_count:]
+def gather_logits(acc, first, labels, before, mass, pick):
+    wanted = labels - first
+    lane = lax.broadcasted_iota(jnp.int32, before.shape, 1)
+    groups = [acc[:, g : g + LANES] for g in range(0, acc.shape[1], LANES)]
+    now = before
+    for g in groups:
+        now = jnp.maximum(now, g)
+    mass = mass * jnp.exp(before - now)
+    for n, g in enumerate(groups):
+        mass += jnp.exp(g - now)
+        pick += jnp.where(lane == wanted - n * LANES, g, 0.0)
+    return now, mass, pick
+
+
+def score_body(n_out, n_embed, steps_out, carried, scalars_ref, *refs):
+    ctx_ref, other_ref, gain_ref, labels_ref, w_ref, vocab_ref = refs[:6]
+    piece_refs = refs[6 : 6 + n_out]
+    embed_refs = refs[6 + n_out : 6 + n_out + n_embed]
+    refs = refs[6 + n_out + n_embed + carried :]
+    rows_ref, scale_ref, top_ref, mass_ref, pick_ref, squares, joined, weights, embed_s = refs
     j = pl.program_id(0)
     tile = w_ref.shape[1]
     rows = ctx_ref.shape[0]
+    unit = embed_s.shape[0]
+    block = 256 if unit % 256 == 0 else unit
 
     @pl.when(j == 0)
     def _():
-        low = 0
+        joined[:, : ctx_ref.shape[1]] = ctx_ref[...]
+        joined[:, ctx_ref.shape[1] :] = other_ref[...]
+        squares[...] = jnp.zeros(squares.shape, jnp.float32)
+        top_ref[0] = jnp.full(top_ref.shape[1:], NEG, jnp.float32)
+        mass_ref[0] = jnp.zeros(mass_ref.shape[1:], jnp.float32)
+        pick_ref[0] = jnp.zeros(pick_ref.shape[1:], jnp.float32)
+
+    @pl.when(j < steps_out)
+    def _():
+        for n, ref in enumerate(embed_refs):
+            high = ref.shape[0]
+            at = pl.multiple_of(scalars_ref[1 + n_out + n], math.gcd(high, 128))
+            embed_s[pl.ds(at, high), :] = ref[...]
+        local = w_ref.shape[0]
+        weights[:local, :] = w_ref[...]
         for n, ref in enumerate(piece_refs):
             high = ref.shape[0]
-            at = pl.multiple_of(owners_ref[n], 128)
-            turned[:, low : low + high] = other_ref[:, pl.ds(at, high)]
-            low += high
-        squares[...] = jnp.zeros(squares.shape, jnp.float32)
-
-    weights = jnp.concatenate([ref[...] for ref in piece_refs], axis=0)
-    block = 256 if rows % 256 == 0 else rows
-    for lo in range(0, rows, block):
-        acc = jnp.dot(ctx_ref[lo : lo + block, :], w_ref[...], preferred_element_type=jnp.float32)
-        acc += jnp.dot(turned[lo : lo + block, :], weights, preferred_element_type=jnp.float32)
-        acc += embed_ref[lo : lo + block, :].astype(jnp.float32)
-        hidden[j, lo : lo + block, :] = acc
-        part = acc[:, :LANES] * acc[:, :LANES]
-        for g in range(LANES, tile, LANES):
-            part += acc[:, g : g + LANES] * acc[:, g : g + LANES]
-        squares[lo : lo + block, :] += part
-
-    @pl.when(j == pl.num_programs(0) - 1)
-    def _():
-        steps = hidden.shape[0]
-        mean = jnp.sum(squares[...], axis=1, keepdims=True) / (steps * tile)
-        scale = lax.rsqrt(mean + EPSILON)
-        for n in range(steps):
-            out_ref[:, n * tile : (n + 1) * tile] = (
-                hidden[n] * scale * gain_ref[:, n * tile : (n + 1) * tile]
-            ).astype(jnp.bfloat16)
-
-
-def out_project(ctx, other, embed, gain, w_own, pieces, offsets):
-    total, depth = ctx.shape
+            weights[pl.ds(pl.multiple_of(local + scalars_ref[1 + n], 128), high), :] = ref[...]
+        for lo in range(0, rows, block):
+            acc = jnp.dot(joined[lo : lo + block, :], weights[...], preferred_element_type=jnp.float32)
+            acc += embed_s[lo % unit : lo % unit + block, :].astype(jnp.float32)
+            at = pl.ds(pl.multiple_of(j * tile, LANES), tile)
+            rows_ref[0, lo : lo + block, at] = (acc * gain_ref[...]).astype(jnp.bfloat16)
+            part = squares[lo : lo + block, :]
+            for g in range(0, tile, LANES):
+                part += acc[:, g : g + LANES] * acc[:, g : g + LANES]
+            squares[lo : lo + block, :] = part
+
+    @pl.when(j == steps_out - 1)
+    def _():
+        mean = jnp.sum(squares[...], axis=1, keepdims=True) / (steps_out * tile)
+        scale_ref[0] = jnp.broadcast_to(lax.rsqrt(mean + EPSILON), squares.shape)
+
+    @pl.when(j >= steps_out)
+    def _():
+        first = scalars_ref[0] + (j - steps_out) * vocab_ref.shape[1]
+        for lo in range(0, rows, block):
+            at = slice(lo, lo + block)
+            acc = jnp.dot(rows_ref[0, at, :], vocab_ref[...], preferred_element_type=jnp.float32)
+            acc = acc * scale_ref[0, at, :1]
+            top_ref[0, at, :], mass_ref[0, at, :], pick_ref[0, at, :] = gather_logits(
+                acc, first, labels_ref[at, :], top_ref[0, at, :], mass_ref[0, at, :], pick_ref[0, at, :]
+            )
+
+
+def score_own(index, count, before, ctx, other, gain, labels, w_own, w_vocab, pieces, embeds, scalars):
+    rows, depth = ctx.shape
     width = w_own.shape[1]
     tile = largest_tile(width, 512)
-    rows = total
-    line = lambda j, *_: (0, 0)
-    column = lambda j, *_: (0, j)
+    steps_out = width // tile
+    vocab_tile = largest_tile(w_vocab.shape[1], 512)
+    unit = sum(e.shape[0] for e in embeds)
+    fixed = lambda j, *_: (0, 0)
+    column = lambda j, *_: (0, jnp.minimum(j, steps_out - 1))
+    mine = lambda j, *_: (index, 0, 0)
+    shapes = [((count, rows, width), jnp.bfloat16)] + [((count, rows, LANES), jnp.float32)] * 4
     return pl.pallas_call(
-        functools.partial(out_body, len(pieces)),
+        functools.partial(score_body, len(pieces), len(embeds), steps_out, len(before)),
         grid_spec=pltpu.PrefetchScalarGridSpec(
             num_scalar_prefetch=1,
-            grid=(width // tile,),
+            grid=(steps_out + w_vocab.shape[1] // vocab_tile,),
             in_specs=[
-                pl.BlockSpec((rows, depth), line),
-                pl.BlockSpec((rows, other.shape[1]), line),
-                pl.BlockSpec((rows, tile), lambda j, *_: (0, j)),
-                pl.BlockSpec((1, width), lambda j, *_: (0, 0)),
+                pl.BlockSpec((rows, depth), fixed),
+                pl.BlockSpec((rows, other.shape[1]), fixed),
+                pl.BlockSpec((1, tile), column),
+                pl.BlockSpec((rows, 1), fixed),
                 pl.BlockSpec((w_own.shape[0], tile), column),
+                pl.BlockSpec((width, vocab_tile), lambda j, *_: (0, jnp.maximum(j - steps_out, 0))),
             ]
-            + [pl.BlockSpec((piece.shape[0], tile), column) for piece in pieces],
-            out_specs=pl.BlockSpec((rows, width), line),
+            + [pl.BlockSpec((piece.shape[0], tile), column) for piece in pieces]
+            + [pl.BlockSpec((e.shape[0], tile), column) for e in embeds]
+            + [pl.BlockSpec(memory_space=pl.ANY)] * len(before),
+            out_specs=[pl.BlockSpec((1, rows, width), mine)] + [pl.BlockSpec((1, rows, LANES), mine)] * 4,
             scratch_shapes=[
-                pltpu.VMEM((width // tile, rows, tile), jnp.float32),
                 pltpu.VMEM((rows, LANES), jnp.float32),
-                pltpu.VMEM((rows, other.shape[1]), jnp.bfloat16),
+                pltpu.VMEM((rows, depth + other.shape[1]), jnp.bfloat16),
+                pltpu.VMEM((depth + other.shape[1], tile), jnp.bfloat16),
+                pltpu.VMEM((unit, tile), jnp.bfloat16),
             ],
         ),
-        out_shape=jax.ShapeDtypeStruct((total, width), jnp.bfloat16),
+        out_shape=[jax.ShapeDtypeStruct(*shape) for shape in shapes],
+        input_output_aliases={7 + len(pieces) + len(embeds) + n: n for n in range(len(before))},
         cost_estimate=pl.CostEstimate(
-            flops=2 * total * (depth + other.shape[1]) * width, bytes_accessed=4 * depth * width, transcendentals=0
-        ),
-        name="out_project",
-    )(offsets, ctx, other, embed, gain.reshape(1, -1), w_own, *pieces)
-
-
-def vocab_body(piece_count, scalars_ref, rows_ref, labels_ref, top_in, mass_in, pick_in, *rest):
+            flops=2 * rows * width * (depth + other.shape[1] + w_vocab.shape[1]),
+            bytes_accessed=2 * width * (2 * depth + w_vocab.shape[1]),
+            transcendentals=0,
+        ),
+        name="score_own",
+    )(scalars, ctx, other, gain.reshape(1, -1), labels.reshape(-1, 1), w_own, w_vocab, *pieces, *embeds, *before)
+
+
+def far_body(piece_count, scalars_ref, rows_ref, scale_ref, labels_ref, top_in, mass_in, pick_in, *rest):
     piece_refs = rest[:piece_count]
-    top_ref, mass_ref, pick_ref = rest[piece_count:]
-    j = pl.program_id(0)
-    tile = piece_refs[0].shape[1]
+    top_ref, mass_ref, pick_ref, weights = rest[piece_count:]
     rows = rows_ref.shape[0]
-
-    @pl.when(j == 0)
-    def _():
-        top_ref[...] = top_in[...]
-        mass_ref[...] = mass_in[...]
-        pick_ref[...] = pick_in[...]
-
-    first = scalars_ref[0] + j * tile
     block = 256 if rows % 256 == 0 else rows
-    for lo in range(0, rows, block):
-        acc = None
+
+    @pl.when(pl.program_id(0) == 0)
+    def _():
         for n, ref in enumerate(piece_refs):
             high = ref.shape[0]
-            if piece_count == 1:
-                left = rows_ref[lo : lo + block, :]
-            else:
-                at = pl.multiple_of(scalars_ref[1 + n], 128)
-                left = rows_ref[lo : lo + block, pl.ds(at, high)]
-            part = jnp.dot(left, ref[...], preferred_element_type=jnp.float32)
-            acc = part if acc is None else acc + part
-        wanted = labels_ref[lo : lo + block, :] - first
-        lane = lax.broadcasted_iota(jnp.int32, (block, LANES), 1)
-        groups = [acc[:, g : g + LANES] for g in range(0, tile, LANES)]
-        before = top_ref[lo : lo + block, :]
-        now = before
-        for g in groups:
-            now = jnp.maximum(now, g)
-        mass = mass_ref[lo : lo + block, :] * jnp.exp(before - now)
-        pick = pick_ref[lo : lo + block, :]
-        for n, g in enumerate(groups):
-            mass += jnp.exp(g - now)
-            pick += jnp.where(lane == wanted - n * LANES, g, 0.0)
-        top_ref[lo : lo + block, :] = now
-        mass_ref[lo : lo + block, :] = mass
-        pick_ref[lo : lo + block, :] = pick
-
-
-def vocab_stats(normed, labels, pieces, scalars, stats):
-    rows, depth = normed.shape
+            weights[pl.ds(pl.multiple_of(scalars_ref[1 + n], 128), high), :] = ref[...]
+
+    for lo in range(0, rows, block):
+        at = slice(lo, lo + block)
+        acc = jnp.dot(rows_ref[at, :], weights[...], preferred_element_type=jnp.float32)
+        acc = acc * scale_ref[at, :1]
+        top_ref[at, :], mass_ref[at, :], pick_ref[at, :] = gather_logits(
+            acc, scalars_ref[0], labels_ref[at, :], top_in[at, :], mass_in[at, :], pick_in[at, :]
+        )
+
+
+def score_far(rows, scale, labels, stats, pieces, scalars):
+    total, depth = rows.shape
     width = pieces[0].shape[1]
-    tile = largest_tile(width, 512)
-    fixed = lambda j, *_: (0, 0)
-    lanes = pl.BlockSpec((rows, LANES), fixed)
+    block = math.gcd(total, 512)
+    line = lambda i, *_: (i, 0)
+    lanes = pl.BlockSpec((block, LANES), line)
     return pl.pallas_call(
-        functools.partial(vocab_body, len(pieces)),
+        functools.partial(far_body, len(pieces)),
         grid_spec=pltpu.PrefetchScalarGridSpec(
             num_scalar_prefetch=1,
-            grid=(width // tile,),
-            in_specs=[pl.BlockSpec((rows, depth), fixed), pl.BlockSpec((rows, 1), fixed)]
+            grid=(total // block,),
+            in_specs=[pl.BlockSpec((block, depth), line), lanes, pl.BlockSpec((block, 1), line)]
             + [lanes] * 3
-            + [pl.BlockSpec((piece.shape[0], tile), lambda j, *_: (0, j)) for piece in pieces],
+            + [pl.BlockSpec(piece.shape, lambda i, *_: (0, 0)) for piece in pieces],
             out_specs=[lanes] * 3,
-        ),
-        out_shape=[jax.ShapeDtypeStruct((rows, LANES), jnp.float32)] * 3,
+            scratch_shapes=[pltpu.VMEM((depth, width), jnp.bfloat16)],
+        ),
+        out_shape=[jax.ShapeDtypeStruct((total, LANES), jnp.float32)] * 3,
         cost_estimate=pl.CostEstimate(
-            flops=2 * rows * depth * width, bytes_accessed=2 * depth * width, transcendentals=0
-        ),
-        name="vocab_stats",
-    )(scalars, normed, labels.reshape(-1, 1), *stats, *pieces)
-
-
-def fresh_stats(rows):
-    zero = jnp.zeros((rows, LANES), jnp.float32)
-    return (jnp.full((rows, LANES), NEG, jnp.float32), zero, zero)
+            flops=2 * total * depth * width, bytes_accessed=2 * depth * (width + total), transcendentals=0
+        ),
+        name="score_far",
+    )(scalars, rows, scale, labels.reshape(-1, 1), *stats, *pieces)
 
 
 def fold_lanes(stats):
@@ -393,6 +420,8 @@
     stride = 2 if paired else 1
     unit = seq_count * target_len
 
+    flat_labels = labels.reshape(-1)
+    pair_labels = swap_pair(flat_labels, "dp") if paired else None
     got_out = []
     for k in hops:
         got_out.append(shift_by(peer_piece(w_out, "prompt"), "mp", k))
@@ -416,8 +445,7 @@
         + [jnp.arange(pad_len, dtype=jnp.int32)] * prompts_here
     )
     cosine, sine = rope_tables(positions)
-    padded = jnp.pad(prompts, ((0, 0), (0, pad_len - prompt_len), (0, 0))).reshape(-1, model_width)
-    qkv = project(flat_embed, padded, attn_gain, w_qkv, cosine, sine)
+    qkv = project(flat_embed, prompts, pad_len, attn_gain, w_qkv, cosine, sine)
     ctx = attend(qkv, prompts_here, target_len, seq_count, prompt_len, pad_len)
     ctx = ctx.reshape(prompts_here * unit, -1)
 
@@ -435,8 +463,6 @@
         for piece, owner in held:
             out_pieces.append(piece)
             out_offsets.append(n * w_out.shape[0] + owner * piece.shape[0])
-    out_offsets = jnp.stack(out_offsets).astype(jnp.int32)
-
     vocab_sets = []
     for n, got in enumerate(got_vocab):
         held = spread(got, "prompt")
@@ -448,27 +474,38 @@
     def tiled(flat):
         return jnp.tile(flat, (prompts_here,) + (1,) * (flat.ndim - 1))
 
-    own_first = ((my_seq * n_model + lax.axis_index("mp")) * w_vocab.shape[1]).astype(jnp.int32)
-    own_scalars = jnp.stack([own_first, jnp.int32(0)])
-    sets = []
-    rows = out_project(ctx, other_a, tiled(flat_embed), final_gain, w_out, out_pieces, out_offsets)
-    ids = tiled(labels.reshape(-1))
-    stats = vocab_stats(rows, ids, [w_vocab], own_scalars, fresh_stats(rows.shape[0]))
-    sets.append([rows, ids, stats])
+    def numbers(values):
+        return jnp.stack([jnp.asarray(v, jnp.int32) for v in values])
+
+    own_first = (my_seq * n_model + lax.axis_index("mp")) * w_vocab.shape[1]
+    count = 2 if paired else 1
+    ids = [tiled(flat_labels)]
+    got = score_own(
+        0, count, [], ctx, other_a, final_gain, ids[0], w_out, w_vocab, out_pieces, [flat_embed],
+        numbers([own_first] + out_offsets + [0]),
+    )
     if paired:
         other_b = jnp.concatenate([shift_by(ctx_pair, "mp", k) for k in hops], axis=1)
-        embed_pair = assemble(spread(got_embed, "prompt"))
-        ids = tiled(swap_pair(labels.reshape(-1), "dp"))
-        rows = out_project(ctx_pair, other_b, tiled(embed_pair), final_gain, w_out, out_pieces, out_offsets)
-        stats = vocab_stats(rows, ids, [w_vocab], own_scalars, fresh_stats(rows.shape[0]))
-        sets.append([rows, ids, stats])
+        held = spread(got_embed, "prompt")
+        height = got_embed.shape[0]
+        if height % LANES:
+            held = [(assemble(held), 0)]
+        ids.append(tiled(pair_labels))
+        got = score_own(
+            1, count, list(got), ctx_pair, other_b, final_gain, ids[1], w_out, w_vocab, out_pieces,
+            [p for p, _ in held],
+            numbers([own_first] + out_offsets + [o * height for _, o in held]),
+        )
+    rows, scale, *stats = [v.reshape((-1,) + v.shape[2:]) for v in got]
+    every_id = jnp.concatenate(ids)
     for pieces, scalars in vocab_sets:
-        for entry in sets:
-            entry[2] = vocab_stats(entry[0], entry[1], pieces, scalars, entry[2])
-
-    merged = fold_lanes(sets[0][2])
+        stats = score_far(rows, scale, every_id, stats, pieces, scalars)
+
+    folded = fold_lanes(stats)
+    half = folded.shape[1] // count
+    merged = folded[:, :half]
     if paired:
-        merged = combine_stats(merged, swap_pair(fold_lanes(sets[1][2]), "dp"))
+        merged = combine_stats(merged, swap_pair(folded[:, half:], "dp"))
     for other in [shift_by(merged, "mp", k) for k in hops]:
         merged = combine_stats(merged, other)
     losses = merged[0] + jnp.log(merged[1]) - merged[2]

time: 520 us -> 489 us (0.940)
  Pallas kernels: 252 us -> 210 us
  waiting for transfers between devices: 165 us -> 201 us
  local copies, waits for them, and re-layouts: 44.6 us -> 24.1 us
    ppermute x14, waiting for transfers between devices: 121 us -> 164 us  [shift_by(): lax.ppermute(value, axis, [(i, (i + hop) % size) for i in range(size)])]
    pallas_call x12 -> x6, Pallas kernels: 212 us -> 170 us  [the longest x2 104 us: score_own(): pl.pallas_call(functools.partial(score_body, len(pieces), len(embeds), st...]
    ppermute x18, waiting for transfers between devices: 42.7 us -> 14.2 us  [spread(): lax.ppermute(part, axis, pairs)]
    ppermute x4, waiting for transfers between devices: 1.66 us -> 22.9 us  [swap_pair(): return lax.ppermute(value, axis, [(i, i ^ 1) for i in range(size)])]
    another operation x5 -> x2, local copies, waits for them, and re-layouts: 15 us -> 1.2 us  [numbers(): return jnp.stack([jnp.asarray(v, jnp.int32) for v in values])]
    dynamic_update_slice x4 -> x0, local copies, waits for them, and re-layouts: 9.34 us -> none  [assemble(): whole = lax.dynamic_update_slice_in_dim(whole, part, owner * height, 0)]
  transfers between devices with their start and end apart: 36 -> 36, of which waited for: 13 -> 13; matrix products, arithmetic and copies ran while one was open for 7% -> 4% of each run, Pallas kernels for 28% -> 40%
where the time goes in v1:
time: 489 us; the launch traced here: 485 us
  Pallas kernels  210 us (43%)
  waiting for transfers between devices  201 us (41%)
  starting transfers between devices  39.6 us (8%)
  local copies, waits for them, and re-layouts  24.1 us (5%)
  other arithmetic  8.6 us (2%)
    ppermute x14, waiting for transfers between devices, shift_by(): lax.ppermute(value, axis, [(i, (i + hop) % size) for i in range(size)])  164 us
    pallas_call x2, Pallas kernels, score_own(): pl.pallas_call(functools.partial(score_body, len(pieces), len(embeds), st...  104 us
    pallas_call x4, Pallas kernels, score_far(): pl.pallas_call(functools.partial(far_body, len(pieces)), grid_spec=pltpu....  65.5 us
    pallas_call x1, Pallas kernels, project(): pl.pallas_call(functools.partial(qkv_body, rows_target), grid=(3, width /...  27.7 us
    ppermute x4, waiting for transfers between devices, swap_pair(): return lax.ppermute(value, axis, [(i, i ^ 1) for i in range(size)])  22.9 us
    ppermute x14, starting transfers between devices, shift_by(): lax.ppermute(value, axis, [(i, (i + hop) % size) for i in range(size)])  21.9 us
    ppermute x18, waiting for transfers between devices, spread(): lax.ppermute(part, axis, pairs)  14.2 us
    ppermute x18, starting transfers between devices, spread(): lax.ppermute(part, axis, pairs)  13.7 us
  transfers between devices with their start and end apart: 36, of which 13 were waited for; matrix products, arithmetic and copies ran while one was open for 4% of the time, Pallas kernels for 40%

profile of v1, /device:TPU:1, one launch (start us, length us, event | category | flops | bytes accessed | tf_op | source)
XLA Modules:
  0.0 485.1 jit_solution(5749650780006445846)
XLA Ops:
  0.6 1.7 constant_dynamic-slice_fusion.1
  2.4 2.1 collective-permute-start.3
  4.5 2.3 dynamic-slice_bitcast_fusion
  6.8 1.3 collective-permute-start.7
  8.1 4.1 fusion.8
  12.2 2.3 collective-permute-start.12
  14.5 2.2 copy.17.prompt_ref
  16.8 1.4 fusion
  18.2 1.2 pad_maximum_fusion
  19.4 30.5 %collective-permute-done.3.refs_6_ = bf16[256,4096]{1,0:T(8,128)(2,1)} collective-permute-done((bf16[256,4096]{1,0:T(8,128)(2,1)S(1)}, bf16[256,4096]{1,0:T(8,128)(2,1)}, u32[]{:S(2)}, u32[]{:S(2)}) %collective-permute-start.3) | collective-permute-done | bytes 2097184 | tf_op jit(solution)/shard_map/ppermute | solution.py:21
  49.9 1.2 collective-permute-start.4
  51.1 27.7 %qkv_rope.1.q_ref.k_ref.v_ref = bf16[3,768,1024]{2,1,0:T(8,128)(2,1)} custom-call(bf16[512,4096]{1,0:T(8,128)(2,1)} %bitcast.75, bf16[2,100,4096]{2,1,0:T(8,128)(2,1)} %copy.17.prompt_ref, f32[1,4096]{1,0:T(1,128)} %bitcast.104, bf16[3,4096,1024]{2,1,0:T(8,128)(2,1)} %w_ref.1, f32[768,128]{1,0:T(8,128)} %get-tuple-element.70.cos_ref, ...), custom_call_target="tpu_custom_call" | custom-call | flops 19327352832 | bytes 25165824 | tf_op jit(solution)/shard_map/qkv_rope/pallas_call | solution.py:150
  78.8 12.6 %attend.1 = bf16[2,512,1024]{2,1,0:T(8,128)(2,1)} custom-call(bf16[3,768,1024]{2,1,0:T(8,128)(2,1)} %qkv_rope.1.q_ref.k_ref.v_ref, bf16[3,768,1024]{2,1,0:T(8,128)(2,1)} %qkv_rope.1.q_ref.k_ref.v_ref, bf16[3,768,1024]{2,1,0:T(8,128)(2,1)} %qkv_rope.1.q_ref.k_ref.v_ref), custom_call_target="tpu_custom_call" | custom-call | flops 2684354560 | bytes 6291456 | tf_op jit(solution)/shard_map/attend/pallas_call | solution.py:215
  91.4 1.2 collective-permute-start.11
  92.6 1.3 collective-permute-start.2
  93.9 1.5 collective-permute-done.2
  95.4 2.3 collective-permute-start.16
  97.8 2.3 collective-permute-start.24
  100.1 87.8 %collective-permute-done.16.rest_0_ = bf16[1024,512]{1,0:T(8,128)(2,1)} collective-permute-done((bf16[1024,512]{1,0:T(8,128)(2,1)S(1)}, bf16[1024,512]{1,0:T(8,128)(2,1)}, u32[]{:S(2)}, u32[]{:S(2)}) %collective-permute-start.16) | collective-permute-done | bytes 1048608 | tf_op jit(solution)/shard_map/ppermute | solution.py:21
  187.9 1.3 collective-permute-start
  189.2 21.1 %collective-permute-done.20.rest_0_ = bf16[1024,512]{1,0:T(8,128)(2,1)S(1)} collective-permute-done((bf16[1024,512]{1,0:T(8,128)(2,1)S(1)}, bf16[1024,512]{1,0:T(8,128)(2,1)S(1)}, u32[]{:S(2)}, u32[]{:S(2)}) %collective-permute-start.20) | collective-permute-done | bytes 1048608 | tf_op jit(solution)/shard_map/ppermute | solution.py:21
  210.3 1.0 copy-done.6
  211.3 2.7 collective-permute-start.5
  214.0 18.9 %collective-permute-done.24.rest_0_ = bf16[1024,512]{1,0:T(8,128)(2,1)} collective-permute-done((bf16[1024,512]{1,0:T(8,128)(2,1)S(1)}, bf16[1024,512]{1,0:T(8,128)(2,1)}, u32[]{:S(2)}, u32[]{:S(2)}) %collective-permute-start.24) | collective-permute-done | bytes 1048608 | tf_op jit(solution)/shard_map/ppermute | solution.py:21
  233.2 1.8 collective-permute-start.9
  235.0 1.0 copy.27
  236.1 0.6 stack.156.scalars_ref
  236.7 0.6 stack.154.scalars_ref
  237.3 0.6 stack.152.scalars_ref
  237.9 0.7 stack.139.scalars_ref
  238.6 0.6 stack.150.scalars_ref
  239.2 0.6 stack.149.scalars_ref
  239.9 1.0 copy.25
  240.9 1.4 copy.23.labels_ref
  242.3 14.1 %collective-permute-done.8.refs_11_ = bf16[128,4096]{1,0:T(8,128)(2,1)} collective-permute-done((bf16[128,4096]{1,0:T(8,128)(2,1)}, bf16[128,4096]{1,0:T(8,128)(2,1)}, u32[]{:S(2)}, u32[]{:S(2)}) %collective-permute-start.8) | collective-permute-done | bytes 1048608 | tf_op jit(solution)/shard_map/ppermute | solution.py:51
  256.6 2.7 collective-permute-start.14
  259.3 19.5 %collective-permute-done.refs_0_ = bf16[1024,1024]{1,0:T(8,128)(2,1)} collective-permute-done((bf16[1024,1024]{1,0:T(8,128)(2,1)}, bf16[1024,1024]{1,0:T(8,128)(2,1)}, u32[]{:S(2)}, u32[]{:S(2)}) %collective-permute-start) | collective-permute-done | bytes 2097184 | tf_op jit(solution)/shard_map/ppermute | solution.py:409
  279.1 0.8 collective-permute-start.10
  280.2 52.4 %score_own.2 = (bf16[2,1024,4096]{2,1,0:T(8,128)(2,1)}, f32[2,1024,128]{2,1,0:T(8,128)}, f32[2,1024,128]{2,1,0:T(8,128)}, f32[2,1024,128]{2,1,0:T(8,128)}, f32[2,1024,128]{2,1,0:T(8,128)}) custom-call(s32[6]{0:T(128)} %stack.150.scalars_ref, bf16[1024,1024]{1,0:T(8,128)(2,1)} %bitcast.72, bf16[1024,1024]{1,0:T(8,128)(2,1)} %collective-permute-done.11.refs_1_, ...), custom_call_target="tpu_custom_call" | custom-call | flops 34359738368 | bytes 33554432 | tf_op jit(solution)/shard_map/score_own/pallas_call | solution.py:314
  332.9 1.1 collective-permute-start.21
  334.4 0.7 collective-permute-start.15
  335.2 1.3 copy-done.5
  336.5 51.9 %score_own.3 = (bf16[2,1024,4096]{2,1,0:T(8,128)(2,1)}, f32[2,1024,128]{2,1,0:T(8,128)}, f32[2,1024,128]{2,1,0:T(8,128)}, f32[2,1024,128]{2,1,0:T(8,128)}, f32[2,1024,128]{2,1,0:T(8,128)}) custom-call(s32[9]{0:T(128)} %stack.149.scalars_ref, ...), custom_call_target="tpu_custom_call", output_to_operand_aliasing={{0}: (15, {}), {1}: (16, {}), {2}: (17, {}), {3}: (18, {}),... | custom-call | flops 34359738368 | bytes 33554432 | tf_op jit(solution)/shard_map/score_own/pallas_call | solution.py:314
  389.0 16.3 %score_far.4 = (f32[2048,128]{1,0:T(8,128)}, f32[2048,128]{1,0:T(8,128)}, f32[2048,128]{1,0:T(8,128)}) custom-call(s32[5]{0:T(128)} %stack.156.scalars_ref, bf16[2048,4096]{1,0:T(8,128)(2,1)} %bitcast.107, f32[2048,128]{1,0:T(8,128)} %bitcast.111, s32[2048,1]{1,0:T(8,128)} %copy.23.labels_ref, f32[2048,128]{1,0:T(8,128)} %bitcast.115, ...), custom_call_target="tpu_custom_call" | custom-call | flops 8589934592 | bytes 20971520 | tf_op jit(solution)/shard_map/score_far/pallas_call | solution.py:376
  405.9 16.3 %score_far.5 = (f32[2048,128]{1,0:T(8,128)}, f32[2048,128]{1,0:T(8,128)}, f32[2048,128]{1,0:T(8,128)}) custom-call(s32[5]{0:T(128)} %stack.154.scalars_ref, bf16[2048,4096]{1,0:T(8,128)(2,1)} %bitcast.108, f32[2048,128]{1,0:T(8,128)} %bitcast.112, s32[2048,1]{1,0:T(8,128)} %copy.23.labels_ref, f32[2048,128]{1,0:T(8,128)} %get-tuple-element.35.top_in, ...), custom_call_target="tpu_custom_call" | custom-call | flops 8589934592 | bytes 20971520 | tf_op jit(solution)/shard_map/score_far/pallas_call | solution.py:376
  422.3 1.0 copy-done.9
  423.3 16.5 %score_far.6 = (f32[2048,128]{1,0:T(8,128)}, f32[2048,128]{1,0:T(8,128)}, f32[2048,128]{1,0:T(8,128)}) custom-call(s32[5]{0:T(128)} %stack.152.scalars_ref, bf16[2048,4096]{1,0:T(8,128)(2,1)} %bitcast.109, f32[2048,128]{1,0:T(8,128)} %bitcast.113, s32[2048,1]{1,0:T(8,128)} %copy.23.labels_ref, f32[2048,128]{1,0:T(8,128)} %get-tuple-element.38.top_in, ...), custom_call_target="tpu_custom_call" | custom-call | flops 8589934592 | bytes 20971520 | tf_op jit(solution)/shard_map/score_far/pallas_call | solution.py:376
  439.8 0.9 copy-done.10
  440.8 16.3 %score_far.7 = (f32[2048,128]{1,0:T(8,128)}, f32[2048,128]{1,0:T(8,128)}, f32[2048,128]{1,0:T(8,128)}) custom-call(s32[5]{0:T(128)} %stack.139.scalars_ref, bf16[2048,4096]{1,0:T(8,128)(2,1)} %bitcast.110, f32[2048,128]{1,0:T(8,128)} %bitcast.114, s32[2048,1]{1,0:T(8,128)} %copy.23.labels_ref, f32[2048,128]{1,0:T(8,128)} %get-tuple-element.41.top_in, ...), custom_call_target="tpu_custom_call" | custom-call | flops 8589934592 | bytes 20971520 | tf_op jit(solution)/shard_map/score_far/pallas_call | solution.py:376
  457.1 1.7 reduce_max.9
  458.7 2.2 multiply_reduce_fusion
  462.0 1.9 collective-permute-done.28
  464.0 1.2 collective-permute-start.29
  465.3 1.4 collective-permute-done.29
  466.7 0.6 fusion.7
  467.4 3.4 collective-permute-start.31
  470.8 0.9 collective-permute-start.32
  471.8 1.4 collective-permute-done.32
  473.9 5.2 %collective-permute-start.33 = (f32[3]{0:T(128)S(1)}, f32[3]{0:T(128)S(1)}, u32[]{:S(2)}, u32[]{:S(2)}) collective-permute-start(f32[3]{0:T(128)S(1)} %select_reduce_fusion), channel_id=1, source_target_pairs={{0,8},{8,16},{16,24},{24,0},{1,9},{9,17},{17,25},{25,1},{2,10},{10... | collective-permute-start | bytes 44 | tf_op jit(solution)/shard_map/ppermute | solution.py:21
  479.8 1.7 collective-permute-done.34
  481.5 0.8 collective-permute-done.35
  483.0 0.6 slice.73
  483.6 0.6 slice_divide_fusion
  484.2 0.6 div.11
  (90 shorter events, 6.0 us)
Async XLA Ops:
  2.4 47.6 %collective-permute-start.3 = (bf16[256,4096]{1,0:T(8,128)(2,1)S(1)}, bf16[256,4096]{1,0:T(8,128)(2,1)}, u32[]{:S(2)}, u32[]{:S(2)}) collective-permute-start(bf16[256,4096]{1,0:T(8,128)(2,1)S(1)} %constant_dynamic-slice_fusion.1), channel_id=1, source_target_pairs={{0,1},{1,0},{2,3},{3,2},{4,5},{5,4},{6,7},{7,6},{8,9},{9,8},{10,11... | collective-permute-start | bytes 6291464 | tf_op jit(solution)/shard_map/ppermute | solution.py:21
  6.8 90.9 %collective-permute-start.7 = (bf16[128,4096]{1,0:T(8,128)(2,1)}, bf16[128,4096]{1,0:T(8,128)(2,1)}, u32[]{:S(2)}, u32[]{:S(2)}) collective-permute-start(bf16[128,4096]{1,0:T(8,128)(2,1)} %dynamic-slice_bitcast_fusion), channel_id=1, source_target_pairs={{0,2},{2,0},{4,6},{6,4},{1,3},{3,1},{5,7},{7,5},{8,10},{10,8},{12,... | collective-permute-start | bytes 3145736 | tf_op jit(solution)/shard_map/ppermute | solution.py:409
  8.1 6.4 %copy-start = (bf16[2,100,4096]{2,0,1:T(2,128)(2,1)S(1)}, bf16[2,100,4096]{2,0,1:T(2,128)(2,1)}, u32[]{:S(2)}) copy-start(bf16[2,100,4096]{2,0,1:T(2,128)(2,1)} %param.11) | copy-start | bytes 4915204
  12.2 85.6 %collective-permute-start.12 = (bf16[1024,512]{1,0:T(8,128)(2,1)}, bf16[1024,512]{1,0:T(8,128)(2,1)}, u32[]{:S(2)}, u32[]{:S(2)}) collective-permute-start(bf16[1024,512]{1,0:T(8,128)(2,1)} %get-tuple-element.52), channel_id=1, source_target_pairs={{0,4},{2,6},{4,0},{6,2},{1,5},{3,7},{5,1},{7,3},{8,12},{10,14},{12... | collective-permute-start | bytes 3145736 | tf_op jit(solution)/shard_map/ppermute | solution.py:21
  49.9 164.1 %collective-permute-start.4 = (bf16[256,4096]{1,0:T(8,128)(2,1)}, bf16[256,4096]{1,0:T(8,128)(2,1)}, u32[]{:S(2)}, u32[]{:S(2)}) collective-permute-start(bf16[256,4096]{1,0:T(8,128)(2,1)} %collective-permute-done.3.refs_6_), channel_id=1, source_target_pairs={{0,16},{8,24},{16,0},{24,8},{1,17},{9,25},{17,1},{25,9},{2,18},{10... | collective-permute-start | bytes 6291464 | tf_op jit(solution)/shard_map/ppermute | solution.py:51
  78.8 13.8 %copy-start.4 = (s32[1,512]{1,0:T(1,128)S(1)}, s32[1,512]{1,0:T(1,128)}, u32[]{:S(2)}) copy-start(s32[1,512]{1,0:T(1,128)} %param.13) | copy-start | bytes 6148
  78.8 16.7 %copy-start.2 = (bf16[1024,512]{1,0:T(8,128)(2,1)S(1)}, bf16[1024,512]{1,0:T(8,128)(2,1)}, u32[]{:S(2)}) copy-start(bf16[1024,512]{1,0:T(8,128)(2,1)} %get-tuple-element.51) | copy-start | bytes 3145732
  78.8 19.0 %copy-start.1 = (bf16[1024,512]{1,0:T(8,128)(2,1)S(1)}, bf16[1024,512]{1,0:T(8,128)(2,1)}, u32[]{:S(2)}) copy-start(bf16[1024,512]{1,0:T(8,128)(2,1)} %get-tuple-element.50) | copy-start | bytes 3145732
  91.4 141.8 %collective-permute-start.11 = (bf16[1024,1024]{1,0:T(8,128)(2,1)}, bf16[1024,1024]{1,0:T(8,128)(2,1)}, u32[]{:S(2)}, u32[]{:S(2)}) collective-permute-start(bf16[1024,1024]{1,0:T(8,128)(2,1)} %bitcast.70), channel_id=1, source_target_pairs={{0,1},{1,0},{2,3},{3,2},{4,5},{5,4},{6,7},{7,6},{8,9},{9,8},{10,11... | collective-permute-start | bytes 6291464 | tf_op jit(solution)/shard_map/ppermute | solution.py:21
  92.6 2.8 collective-permute-start.2
  95.4 92.5 %collective-permute-start.16 = (bf16[1024,512]{1,0:T(8,128)(2,1)S(1)}, bf16[1024,512]{1,0:T(8,128)(2,1)}, u32[]{:S(2)}, u32[]{:S(2)}) collective-permute-start(bf16[1024,512]{1,0:T(8,128)(2,1)S(1)} %copy-done.2), channel_id=1, source_target_pairs={{0,4},{2,6},{4,0},{6,2},{1,5},{3,7},{5,1},{7,3},{8,12},{10,14},{12... | collective-permute-start | bytes 3145736 | tf_op jit(solution)/shard_map/ppermute | solution.py:21
  97.8 112.6 %collective-permute-start.20 = (bf16[1024,512]{1,0:T(8,128)(2,1)S(1)}, bf16[1024,512]{1,0:T(8,128)(2,1)S(1)}, u32[]{:S(2)}, u32[]{:S(2)}) collective-permute-start(bf16[1024,512]{1,0:T(8,128)(2,1)S(1)} %copy-done.1), channel_id=1, source_target_pairs={{0,4},{2,6},{4,0},{6,2},{1,5},{3,7},{5,1},{7,3},{8,12},{10,14},{12... | collective-permute-start | bytes 3145736 | tf_op jit(solution)/shard_map/ppermute | solution.py:21
  97.8 135.1 %collective-permute-start.24 = (bf16[1024,512]{1,0:T(8,128)(2,1)S(1)}, bf16[1024,512]{1,0:T(8,128)(2,1)}, u32[]{:S(2)}, u32[]{:S(2)}) collective-permute-start(bf16[1024,512]{1,0:T(8,128)(2,1)S(1)} %get-tuple-element.49), channel_id=1, source_target_pairs={{0,4},{2,6},{4,0},{6,2},{1,5},{3,7},{5,1},{7,3},{8,12},{10,14},{12... | collective-permute-start | bytes 3145736 | tf_op jit(solution)/shard_map/ppermute | solution.py:21
  187.9 90.9 %collective-permute-start = (bf16[1024,1024]{1,0:T(8,128)(2,1)}, bf16[1024,1024]{1,0:T(8,128)(2,1)}, u32[]{:S(2)}, u32[]{:S(2)}) collective-permute-start(bf16[1024,1024]{1,0:T(8,128)(2,1)} %bitcast.71), channel_id=1, source_target_pairs={{0,2},{2,0},{4,6},{6,4},{1,3},{3,1},{5,7},{7,5},{8,10},{10,8},{12,... | collective-permute-start | bytes 6291464 | tf_op jit(solution)/shard_map/ppermute | solution.py:409
  210.3 1.0 copy-start.6
  211.3 67.7 %collective-permute-start.5 = (bf16[256,4096]{1,0:T(8,128)(2,1)}, bf16[256,4096]{1,0:T(8,128)(2,1)}, u32[]{:S(2)}, u32[]{:S(2)}) collective-permute-start(bf16[256,4096]{1,0:T(8,128)(2,1)} %collective-permute-done.3.refs_6_), channel_id=1, source_target_pairs={{0,8},{8,0},{16,24},{24,16},{1,9},{9,1},{17,25},{25,17},{2,10},{10... | collective-permute-start | bytes 6291464 | tf_op jit(solution)/shard_map/ppermute | solution.py:51
  214.0 65.8 %collective-permute-start.6 = (bf16[256,4096]{1,0:T(8,128)(2,1)}, bf16[256,4096]{1,0:T(8,128)(2,1)}, u32[]{:S(2)}, u32[]{:S(2)}) collective-permute-start(bf16[256,4096]{1,0:T(8,128)(2,1)} %collective-permute-done.4.refs_7_), channel_id=1, source_target_pairs={{0,8},{8,0},{16,24},{24,16},{1,9},{9,1},{17,25},{25,17},{2,10},{10... | collective-permute-start | bytes 6291464 | tf_op jit(solution)/shard_map/ppermute | solution.py:51
  232.9 23.5 %collective-permute-start.8 = (bf16[128,4096]{1,0:T(8,128)(2,1)}, bf16[128,4096]{1,0:T(8,128)(2,1)}, u32[]{:S(2)}, u32[]{:S(2)}) collective-permute-start(bf16[128,4096]{1,0:T(8,128)(2,1)} %collective-permute-done.7.refs_10_), channel_id=1, source_target_pairs={{0,16},{8,24},{16,0},{24,8},{1,17},{9,25},{17,1},{25,9},{2,18},{10... | collective-permute-start | bytes 3145736 | tf_op jit(solution)/shard_map/ppermute | solution.py:51
  233.2 23.5 %collective-permute-start.9 = (bf16[128,4096]{1,0:T(8,128)(2,1)}, bf16[128,4096]{1,0:T(8,128)(2,1)S(1)}, u32[]{:S(2)}, u32[]{:S(2)}) collective-permute-start(bf16[128,4096]{1,0:T(8,128)(2,1)} %collective-permute-done.7.refs_10_), channel_id=1, source_target_pairs={{0,8},{8,0},{16,24},{24,16},{1,9},{9,1},{17,25},{25,17},{2,10},{10... | collective-permute-start | bytes 3145736 | tf_op jit(solution)/shard_map/ppermute | solution.py:51
  256.4 76.1 %collective-permute-start.13 = (bf16[1024,512]{1,0:T(8,128)(2,1)}, bf16[1024,512]{1,0:T(8,128)(2,1)}, u32[]{:S(2)}, u32[]{:S(2)}) collective-permute-start(bf16[1024,512]{1,0:T(8,128)(2,1)} %collective-permute-done.12.rest_0_), channel_id=1, source_target_pairs={{0,16},{8,24},{16,0},{24,8},{1,17},{9,25},{17,1},{25,9},{2,18},{10... | collective-permute-start | bytes 3145736 | tf_op jit(solution)/shard_map/ppermute | solution.py:51
  256.6 23.5 %copy-start.8 = (bf16[128,4096]{1,0:T(8,128)(2,1)}, bf16[128,4096]{1,0:T(8,128)(2,1)S(1)}, u32[]{:S(2)}) copy-start(bf16[128,4096]{1,0:T(8,128)(2,1)S(1)} %collective-permute-done.9.refs_12_) | copy-start | bytes 3145732
  256.6 76.3 %collective-permute-start.14 = (bf16[1024,512]{1,0:T(8,128)(2,1)}, bf16[1024,512]{1,0:T(8,128)(2,1)}, u32[]{:S(2)}, u32[]{:S(2)}) collective-permute-start(bf16[1024,512]{1,0:T(8,128)(2,1)} %collective-permute-done.12.rest_0_), channel_id=1, source_target_pairs={{0,8},{8,0},{16,24},{24,16},{1,9},{9,1},{17,25},{25,17},{2,10},{10... | collective-permute-start | bytes 3145736 | tf_op jit(solution)/shard_map/ppermute | solution.py:51
  278.8 55.3 %collective-permute-start.17 = (bf16[1024,512]{1,0:T(8,128)(2,1)}, bf16[1024,512]{1,0:T(8,128)(2,1)}, u32[]{:S(2)}, u32[]{:S(2)}) collective-permute-start(bf16[1024,512]{1,0:T(8,128)(2,1)} %collective-permute-done.16.rest_0_), channel_id=1, source_target_pairs={{0,16},{8,24},{16,0},{24,8},{1,17},{9,25},{17,1},{25,9},{2,18},{10... | collective-permute-start | bytes 3145736 | tf_op jit(solution)/shard_map/ppermute | solution.py:51
  279.1 55.3 %collective-permute-start.10 = (bf16[128,4096]{1,0:T(8,128)(2,1)}, bf16[128,4096]{1,0:T(8,128)(2,1)}, u32[]{:S(2)}, u32[]{:S(2)}) collective-permute-start(bf16[128,4096]{1,0:T(8,128)(2,1)} %collective-permute-done.8.refs_11_), channel_id=1, source_target_pairs={{0,8},{8,0},{16,24},{24,16},{1,9},{9,1},{17,25},{25,17},{2,10},{10... | collective-permute-start | bytes 3145736 | tf_op jit(solution)/shard_map/ppermute | solution.py:51
  279.9 55.3 %collective-permute-start.1 = (bf16[1024,1024]{1,0:T(8,128)(2,1)}, bf16[1024,1024]{1,0:T(8,128)(2,1)S(1)}, u32[]{:S(2)}, u32[]{:S(2)}) collective-permute-start(bf16[1024,1024]{1,0:T(8,128)(2,1)} %collective-permute-done.refs_0_), channel_id=1, source_target_pairs={{0,1},{1,0},{2,3},{3,2},{4,5},{5,4},{6,7},{7,6},{8,9},{9,8},{10,11... | collective-permute-start | bytes 6291464 | tf_op jit(solution)/shard_map/ppermute | solution.py:21
  280.1 52.8 %copy-start.7 = (bf16[1024,512]{1,0:T(8,128)(2,1)S(1)}, bf16[1024,512]{1,0:T(8,128)(2,1)}, u32[]{:S(2)}) copy-start(bf16[1024,512]{1,0:T(8,128)(2,1)} %copy-done.6) | copy-start | bytes 3145732
  332.5 72.8 %collective-permute-start.18 = (bf16[1024,512]{1,0:T(8,128)(2,1)}, bf16[1024,512]{1,0:T(8,128)(2,1)}, u32[]{:S(2)}, u32[]{:S(2)}) collective-permute-start(bf16[1024,512]{1,0:T(8,128)(2,1)} %collective-permute-done.16.rest_0_), channel_id=1, source_target_pairs={{0,8},{8,0},{16,24},{24,16},{1,9},{9,1},{17,25},{25,17},{2,10},{10... | collective-permute-start | bytes 3145736 | tf_op jit(solution)/shard_map/ppermute | solution.py:51
  332.9 55.5 %collective-permute-start.21 = (bf16[1024,512]{1,0:T(8,128)(2,1)S(1)}, bf16[1024,512]{1,0:T(8,128)(2,1)}, u32[]{:S(2)}, u32[]{:S(2)}) collective-permute-start(bf16[1024,512]{1,0:T(8,128)(2,1)S(1)} %copy-done.7), channel_id=1, source_target_pairs={{0,16},{8,24},{16,0},{24,8},{1,17},{9,25},{17,1},{25,9},{2,18},{10... | collective-permute-start | bytes 3145736 | tf_op jit(solution)/shard_map/ppermute | solution.py:51
  334.1 71.4 %collective-permute-start.25 = (bf16[1024,512]{1,0:T(8,128)(2,1)}, bf16[1024,512]{1,0:T(8,128)(2,1)}, u32[]{:S(2)}, u32[]{:S(2)}) collective-permute-start(bf16[1024,512]{1,0:T(8,128)(2,1)} %collective-permute-done.24.rest_0_), channel_id=1, source_target_pairs={{0,16},{8,24},{16,0},{24,8},{1,17},{9,25},{17,1},{25,9},{2,18},{10... | collective-permute-start | bytes 3145736 | tf_op jit(solution)/shard_map/ppermute | solution.py:51
  334.4 54.1 %collective-permute-start.15 = (bf16[1024,512]{1,0:T(8,128)(2,1)}, bf16[1024,512]{1,0:T(8,128)(2,1)}, u32[]{:S(2)}, u32[]{:S(2)}) collective-permute-start(bf16[1024,512]{1,0:T(8,128)(2,1)} %collective-permute-done.13.rest_1_), channel_id=1, source_target_pairs={{0,8},{8,0},{16,24},{24,16},{1,9},{9,1},{17,25},{25,17},{2,10},{10... | collective-permute-start | bytes 3145736 | tf_op jit(solution)/shard_map/ppermute | solution.py:51
  335.1 1.4 copy-start.5
  335.1 70.8 %collective-permute-start.19 = (bf16[1024,512]{1,0:T(8,128)(2,1)}, bf16[1024,512]{1,0:T(8,128)(2,1)}, u32[]{:S(2)}, u32[]{:S(2)}) collective-permute-start(bf16[1024,512]{1,0:T(8,128)(2,1)} %collective-permute-done.17.rest_1_), channel_id=1, source_target_pairs={{0,8},{8,0},{16,24},{24,16},{1,9},{9,1},{17,25},{25,17},{2,10},{10... | collective-permute-start | bytes 3145736 | tf_op jit(solution)/shard_map/ppermute | solution.py:51
  388.4 33.8 %collective-permute-start.22 = (bf16[1024,512]{1,0:T(8,128)(2,1)S(1)}, bf16[1024,512]{1,0:T(8,128)(2,1)S(1)}, u32[]{:S(2)}, u32[]{:S(2)}) collective-permute-start(bf16[1024,512]{1,0:T(8,128)(2,1)S(1)} %copy-done.7), channel_id=1, source_target_pairs={{0,8},{8,0},{16,24},{24,16},{1,9},{9,1},{17,25},{25,17},{2,10},{10... | collective-permute-start | bytes 3145736 | tf_op jit(solution)/shard_map/ppermute | solution.py:51
  388.5 33.8 %collective-permute-start.23 = (bf16[1024,512]{1,0:T(8,128)(2,1)}, bf16[1024,512]{1,0:T(8,128)(2,1)}, u32[]{:S(2)}, u32[]{:S(2)}) collective-permute-start(bf16[1024,512]{1,0:T(8,128)(2,1)} %collective-permute-done.21.rest_1_), channel_id=1, source_target_pairs={{0,8},{8,0},{16,24},{24,16},{1,9},{9,1},{17,25},{25,17},{2,10},{10... | collective-permute-start | bytes 3145736 | tf_op jit(solution)/shard_map/ppermute | solution.py:51
  405.3 34.5 %collective-permute-start.26 = (bf16[1024,512]{1,0:T(8,128)(2,1)}, bf16[1024,512]{1,0:T(8,128)(2,1)S(1)}, u32[]{:S(2)}, u32[]{:S(2)}) collective-permute-start(bf16[1024,512]{1,0:T(8,128)(2,1)} %collective-permute-done.24.rest_0_), channel_id=1, source_target_pairs={{0,8},{8,0},{16,24},{24,16},{1,9},{9,1},{17,25},{25,17},{2,10},{10... | collective-permute-start | bytes 3145736 | tf_op jit(solution)/shard_map/ppermute | solution.py:51
  405.5 34.3 %collective-permute-start.27 = (bf16[1024,512]{1,0:T(8,128)(2,1)}, bf16[1024,512]{1,0:T(8,128)(2,1)}, u32[]{:S(2)}, u32[]{:S(2)}) collective-permute-start(bf16[1024,512]{1,0:T(8,128)(2,1)} %collective-permute-done.25.rest_1_), channel_id=1, source_target_pairs={{0,8},{8,0},{16,24},{24,16},{1,9},{9,1},{17,25},{25,17},{2,10},{10... | collective-permute-start | bytes 3145736 | tf_op jit(solution)/shard_map/ppermute | solution.py:51
  422.3 1.0 copy-start.9
  439.8 1.0 copy-start.10
  457.1 3.8 copy-start.3
  461.3 2.7 collective-permute-start.28
  464.0 2.7 collective-permute-start.29
  467.4 4.4 collective-permute-start.30
  467.4 4.4 collective-permute-start.31
  470.8 2.4 collective-permute-start.32
  473.9 5.9 %collective-permute-start.33 = (f32[3]{0:T(128)S(1)}, f32[3]{0:T(128)S(1)}, u32[]{:S(2)}, u32[]{:S(2)}) collective-permute-start(f32[3]{0:T(128)S(1)} %select_reduce_fusion), channel_id=1, source_target_pairs={{0,8},{8,16},{16,24},{24,0},{1,9},{9,17},{17,25},{25,1},{2,10},{10... | collective-permute-start | bytes 44 | tf_op jit(solution)/shard_map/ppermute | solution.py:21
  479.1 2.4 collective-permute-start.34
  479.3 3.0 collective-permute-start.35
